TPU v7x, 128 devices: a whole 4x4x4 slice. The times are simulated.
128 devices in a mesh: span: 8 (over y, core), height: 4 (over x), depth: 4 (over z).
Axes of the slice: x: 4, y: 4, z: 4, core: 2. Of those that a mesh axis runs over, the one named last changes fastest.
Arguments:
- load: float32 [8, 128, 64, 512], P(None, 'span', 'height', 'depth'), may hold values from -6 to 6
- phase: float32 [128, 64, 512], P('span', 'height', 'depth'), may hold values from 0.1 to 1
- void: int32 [16, 8, 64], P('span', 'height', 'depth'), may hold values from 0 to 1, as said below
- owner: int32 [16, 8, 64], P('span', 'height', 'depth'), may hold values from 0 to 7, as said below
- precond: bfloat16 [2048, 512, 512], P(('span', 'height', 'depth')), may hold values from -1 to 2, as said below
Outputs:
- displacement: float32 [8, 128, 64, 512], P(None, 'span', 'height', 'depth')
- sensitivity: float32 [128, 64, 512], P('span', 'height', 'depth')
- phase_next: float32 [128, 64, 512], P('span', 'height', 'depth')
Inputs may be any that keep to these rules, and one draw needn't show every extreme that they name: `void`: each device's block of 16 x 16 x 128 cells holds at most 16 solid bricks; some device holds exactly 16. `owner`: among the solid bricks of one device at most 2 name any one value; on some device every value is named by exactly 2 solid bricks. Values of void bricks carry no meaning. `precond`: every block is symmetric with a positive diagonal that dominates each row.
All inputs are finite; a program needn't handle non-finite values.
Results may differ from a plain program's by a relative error of at most 0.0021.
Values may be sent and summed in bfloat16 or wider, within the bound.
A program may use at most 128 MiB of HBM per device.

v0:
```python
import functools

import jax
import jax.numpy as jnp
from jax import lax
from jax.experimental import pallas as pl
from jax.experimental.pallas import tpu as pltpu
from jax.sharding import PartitionSpec as P

AXES = ("span", "height", "depth")
MESH = pl.DeviceIdType.MESH
F32 = jnp.float32
BF16 = jnp.bfloat16

void_stiffness = 0.001
spring_rate = 0.05
time_step = 0.5
interface_weight = 0.5
epsilon_peak = 1e-06
inverse = 1.0 / (1.0 / time_step + 6.0 * interface_weight)

PITCH = 264

PARTNERS = ((0, 1), (1, 0), (3, 0), (1, 1), (3, 1), (2, 0), (2, 1))
FAR_FIRST = (5, 6, 1, 2, 3, 4, 0)


def block_transpose(rows):
    lane_block = lax.broadcasted_iota(jnp.int32, (8, 128), 1) // 8
    rows = [pltpu.roll(r, 8 * t, 1) if t else r for t, r in enumerate(rows)]
    for bit in (1, 2, 4, 8):
        taken = (lane_block % (2 * bit)) >= bit
        rows = [jnp.where(taken, rows[(t + bit) % 16], rows[t]) for t in range(16)]
    out = []
    for s in range(16):
        r = rows[(16 - s) % 16]
        out.append(pltpu.roll(r, 128 - 8 * s, 1) if s else r)
    return out


def kernel(
    sizes,
    load_hbm, phase_hbm, void_hbm, owner_hbm, precond_hbm,
    disp_hbm, sens_hbm, next_hbm,
    load_v, void_v, owner_v, pre_v, sel, ez, mrow, lb, vs, gbuf,
    send_a, recv_a, send_r, recv_r, field, image, hz_s, hz_r, hz_m, xfield, dx,
    ext, sf_s, sf_r, sf_m, dco, wx, wyp, wym, wzl, wze, base, hpart, erow, sens, nxt, ar_s, ar_r,
    in_sem, pre_sem, out_sem, a2a_ss, a2a_rs, ret_ss, ret_rs, halo_ss, halo_rs,
    sf_ss, sf_rs, ar_ss, ar_rs,
):
    n_span, n_height, n_depth = sizes
    S, H, D = (lax.axis_index(a) for a in AXES)
    yy, core = S // 2, S % 2
    lane = lax.broadcasted_iota(jnp.int32, (8, 128), 1)

    def towards(dy, dc):
        return lax.rem(yy + dy, 4) * 2 + (1 - core if dc else core)

    def back(dy, dc):
        return lax.rem(yy + 4 - dy, 4) * 2 + (1 - core if dc else core)

    load_in = [
        pltpu.make_async_copy(
            load_hbm.at[pl.ds(l * 256, 256)], load_v.at[pl.ds(l * PITCH, 256)], in_sem.at[l]
        )
        for l in range(8)
    ]
    void_in = pltpu.make_async_copy(void_hbm, void_v, in_sem.at[8])
    owner_in = pltpu.make_async_copy(owner_hbm, owner_v, in_sem.at[9])
    phase_in = pltpu.make_async_copy(phase_hbm, ext.at[1, pl.ds(16, 256)], in_sem.at[10])
    void_in.start()
    owner_in.start()
    for c in load_in:
        c.start()
    phase_in.start()

    barrier = pltpu.get_barrier_semaphore()
    for dy, dc in PARTNERS:
        pl.semaphore_signal(barrier, 1, device_id={"span": towards(dy, dc)}, device_id_type=MESH)
    for d in range(1, n_height):
        pl.semaphore_signal(
            barrier, 1, device_id={"height": lax.rem(H + d, n_height)}, device_id_type=MESH
        )
    for d in range(1, n_depth):
        pl.semaphore_signal(
            barrier, 1, device_id={"depth": lax.rem(D + d, n_depth)}, device_id_type=MESH
        )

    sources = [S] + [back(dy, dc) for dy, dc in PARTNERS]
    pre_in = [
        pltpu.make_async_copy(
            precond_hbm.at[pl.ds(src * 2, 2)], pre_v.at[pl.ds(src * 2, 2)], pre_sem.at[n]
        )
        for n, src in enumerate(sources)
    ]
    for c in pre_in:
        c.start()

    void_in.wait()
    owner_in.wait()
    o_row = lax.broadcasted_iota(jnp.int32, (8, 16), 0)
    onehots = []
    for bx in range(2):
        own2, solid2 = owner_v[bx], 1 - void_v[bx]
        for by in range(2):
            own_row = jnp.broadcast_to(own2[by : by + 1, :], (8, 16))
            sol_row = jnp.broadcast_to(solid2[by : by + 1, :], (8, 16))
            onehots.append(jnp.where((own_row == o_row) & (sol_row == 1), 1.0, 0.0))
    onehot = jnp.concatenate(onehots, axis=0)
    b_row = lax.broadcasted_iota(jnp.int32, (16, 128), 0)
    b_lane = lax.broadcasted_iota(jnp.int32, (16, 128), 1) // 8
    spread = jnp.concatenate(
        [
            jnp.where(b_row == b_lane, 1.0, 0.0),
            jnp.where(b_row < b_lane, 1.0, 0.0),
            jnp.ones((16, 128), F32),
        ],
        axis=1,
    )
    counted = jnp.dot(onehot, spread, preferred_element_type=F32)
    o_col = lax.broadcasted_iota(jnp.int32, (8, 128), 0).astype(F32)
    row_id = lax.broadcasted_iota(jnp.int32, (128, 128), 0).astype(F32)
    lane_row = lax.broadcasted_iota(jnp.int32, (1, 128), 1)
    previous = jnp.zeros((8, 128), F32)
    edge = jnp.full((1, 128), -1.0, F32)
    for c in range(4):
        here = counted[c * 8 : c * 8 + 8, 0:128]
        before = counted[c * 8 : c * 8 + 8, 128:256] + previous
        previous = previous + counted[c * 8 : c * 8 + 8, 256:384]
        solid = jnp.sum(here, axis=0, keepdims=True)
        slot = jnp.sum(here * (2.0 * o_col + before), axis=0, keepdims=True)
        code = jnp.where(solid > 0.5, slot * 8.0 + (lane_row % 8).astype(F32), -1.0)
        mrow[c : c + 1, :] = solid
        picked = jnp.where(row_id == code, 1.0, 0.0).astype(BF16)
        sel[0:128, c * 128 : (c + 1) * 128] = picked
        sel[128:256, c * 128 : (c + 1) * 128] = picked
        edge = jnp.where(lane_row % 8 == 2 * c, jnp.broadcast_to(code[:, 127:128], (1, 128)), edge)
        edge = jnp.where(lane_row % 8 == 2 * c + 1, jnp.broadcast_to(code[:, 0:1], (1, 128)), edge)
    picked = jnp.where(row_id == edge, 1.0, 0.0).astype(BF16)
    ez[0:128, :] = picked
    ez[128:256, :] = picked

    def halo_copies(it):
        f = field.at[it]
        inner = pl.ds(1, 16)
        copies = []
        for n, (axis, idx, size, src, dst) in enumerate(
            (
                ("span", S, n_span, f.at[16, inner], f.at[0, inner]),
                ("span", S, n_span, f.at[1, inner], f.at[17, inner]),
                ("height", H, n_height, f.at[inner, 16], f.at[inner, 0]),
                ("height", H, n_height, f.at[inner, 1], f.at[inner, 17]),
                ("depth", D, n_depth, hz_s.at[it], hz_r.at[it, 0]),
                ("depth", D, n_depth, hz_s.at[it], hz_r.at[it, 1]),
            )
        ):
            copies.append((axis, idx, size, n % 2, src, dst, halo_ss.at[it, n], halo_rs.at[it, n]))
        return copies

    def small_copies(e):
        f = ext.at[e]
        copies = []
        for n, (axis, idx, size, src, dst) in enumerate(
            (
                ("span", S, n_span, f.at[pl.ds(256, 16)], f.at[pl.ds(0, 16)]),
                ("span", S, n_span, f.at[pl.ds(16, 16)], f.at[pl.ds(272, 16)]),
                ("height", H, n_height, sf_s.at[e, 1], sf_r.at[e, 0]),
                ("height", H, n_height, sf_s.at[e, 0], sf_r.at[e, 1]),
                ("depth", D, n_depth, sf_s.at[e, 2, pl.ds(0, 8)], sf_r.at[e, 2, pl.ds(0, 8)]),
                ("depth", D, n_depth, sf_s.at[e, 2, pl.ds(0, 8)], sf_r.at[e, 2, pl.ds(8, 8)]),
            )
        ):
            copies.append((axis, idx, size, n % 2, src, dst, sf_ss.at[e, n], sf_rs.at[e, n]))
        return copies

    def make(copy):
        axis, idx, size, direction, src, dst, ss, rs = copy
        target = idx + 1 if direction == 0 else idx - 1
        return pltpu.make_async_remote_copy(
            src_ref=src, dst_ref=dst, send_sem=ss, recv_sem=rs,
            device_id={axis: lax.rem(target + size, size)}, device_id_type=MESH,
        )

    def sends(copy):
        _, idx, size, direction = copy[:4]
        return idx < size - 1 if direction == 0 else idx > 0

    def receives(copy):
        _, idx, size, direction = copy[:4]
        return idx > 0 if direction == 0 else idx < size - 1

    def start_all(copies):
        for copy in copies:
            if copy[2] > 1:
                pl.when(sends(copy))(lambda copy=copy: make(copy).start())

    def receive_all(copies):
        for copy in copies:
            if copy[2] > 1:
                pl.when(receives(copy))(lambda copy=copy: make(copy).wait_recv())

    def sent_all(copies):
        for copy in copies:
            if copy[2] > 1:
                pl.when(sends(copy))(lambda copy=copy: make(copy).wait_send())

    def span_copy(src, dst, ss, rs, partner):
        return pltpu.make_async_remote_copy(
            src_ref=src, dst_ref=dst, send_sem=ss, recv_sem=rs,
            device_id={"span": partner}, device_id_type=MESH,
        )

    def a2a_out(it, n):
        to = towards(*PARTNERS[n])
        return span_copy(
            send_a.at[it, to], recv_a.at[it, S], a2a_ss.at[it, n], a2a_rs.at[it, n], to
        )

    def a2a_back(it, n):
        to = back(*PARTNERS[n])
        return span_copy(
            send_r.at[it, to], recv_r.at[it, S], ret_ss.at[it, n], ret_rs.at[it, n], to
        )

    def ar_copies(k, stage):
        if stage == 0:
            return [
                span_copy(
                    ar_s.at[k, 0], ar_r.at[k, n], ar_ss.at[k, n], ar_rs.at[k, n], towards(*p)
                )
                for n, p in enumerate(PARTNERS)
            ]
        axis, idx, size = (("height", H, n_height), ("depth", D, n_depth))[stage - 1]
        first = 7 if stage == 1 else 10
        return [
            pltpu.make_async_remote_copy(
                src_ref=ar_s.at[k, stage], dst_ref=ar_r.at[k, first + d - 1],
                send_sem=ar_ss.at[k, first + d - 1], recv_sem=ar_rs.at[k, first + d - 1],
                device_id={axis: lax.rem(idx + d, size)}, device_id_type=MESH,
            )
            for d in range(1, size)
        ]

    def ar_begin(k, stage, value):
        ar_s[k, stage] = value
        for c in ar_copies(k, stage):
            c.start()

    def ar_end(k, stage, combine):
        copies = ar_copies(k, stage)
        for c in copies:
            c.wait_recv()
        first = (0, 7, 10)[stage]
        total = ar_s[k, stage]
        for n in range(len(copies)):
            total = combine(total, ar_r[k, first + n])
        return total

    def gather(it, row):
        def pack(i, _):
            for c in range(4):
                bx, by = c // 2, c % 2
                for j in range(0, 8, 2):
                    both = jnp.concatenate(
                        [row(8 * bx + i, 8 * by + j), row(8 * bx + i, 8 * by + j + 1)], axis=0
                    )
                    at = pl.multiple_of(i * 64, 64) + j * 8
                    lb[pl.ds(at, 16), c * 128 : (c + 1) * 128] = both.astype(BF16)
            return 0

        lax.fori_loop(0, 8, pack, 0)
        vs[...] = lax.dot_general(
            lb[...], sel[0:128, :], (((1,), (1,)), ((), ())), preferred_element_type=F32
        )

        def turn(g, _):
            start = pl.multiple_of(g * 128, 128)
            slots = block_transpose([vs[pl.ds(start + 8 * t, 8), :] for t in range(16)])
            for o in range(8):
                send_a[it, o, :, pl.ds(start, 128)] = jnp.concatenate(
                    [slots[2 * o], slots[2 * o + 1]], axis=0
                ).astype(BF16)
            return 0

        lax.fori_loop(0, 4, turn, 0)

    def own_product(it, src, lhs, out):
        for rank in range(2):
            result = jnp.dot(lhs[...], pre_v[src * 2 + rank], preferred_element_type=F32)
            out[rank * 8 : rank * 8 + 8, :] = result[rank * 8 : rank * 8 + 8, :]

    def precondition(it):
        if it == 0:
            pre_in[0].wait()
        own_product(it, S, send_a.at[it, S], recv_r.at[it, S])
        for n in range(7):
            if it == 0:
                pre_in[n + 1].wait()
            src = sources[n + 1]
            a2a_out(it, n).wait_recv()
            own_product(it, src, recv_a.at[it, src], send_r.at[it, src])
            a2a_back(it, n).start()

    def scatter(it):
        for n in range(7):
            a2a_back(it, n).wait_recv()

        def turn(g, _):
            start = pl.multiple_of(g * 128, 128)
            slots = [
                recv_r[it, s // 2, (s % 2) * 8 : (s % 2) * 8 + 8, pl.ds(start, 128)]
                for s in range(16)
            ]
            rows = block_transpose(slots)
            for t in range(0, 16, 2):
                both = jnp.concatenate([rows[t], rows[t + 1]], axis=0)
                high = both.astype(BF16)
                gbuf[pl.ds(start + 8 * t, 16), 0:128] = high
                gbuf[pl.ds(start + 8 * t, 16), 128:256] = (both - high.astype(F32)).astype(BF16)
            return 0

        lax.fori_loop(0, 4, turn, 0)

        def place(g, _):
            start = pl.multiple_of(g * 128, 128)
            chunk = gbuf[pl.ds(start, 128), :]
            cells = jnp.dot(chunk, sel[...], preferred_element_type=F32)
            faces = jnp.dot(chunk, ez[...], preferred_element_type=F32)
            packed = jnp.zeros((8, 128), F32)
            for t in range(16):
                ii, j = t // 8, t % 8
                for c in range(4):
                    bx, by = c // 2, c % 2
                    field[it, 1 + 8 * bx + 2 * g + ii, 1 + 8 * by + j] = cells[
                        t * 8 : t * 8 + 8, c * 128 : (c + 1) * 128
                    ]
                packed = jnp.where(lane // 8 == t, faces[t * 8 : t * 8 + 8, :], packed)
            hz_s[it, g] = packed
            return 0

        lax.fori_loop(0, 4, place, 0)

    def merge(right, left):
        return jnp.where(lane % 2 == 0, pltpu.roll(right, 127, 1), pltpu.roll(left, 1, 1))

    def small_faces(e):
        for side, y in ((0, 0), (1, 15)):
            sf_s[e, side] = ext[e, pl.ds(16 + y, 16, stride=16), :]

        def pack(x, packed):
            for h in range(2):
                n = x * 2 + h
                rows = ext[e, pl.ds(pl.multiple_of(x * 16 + 16, 8) + 8 * h, 8), :]
                packed = jnp.where(lane // 2 == n, pltpu.roll(rows, 2 * n + 1, 1), packed)
            return packed

        sf_s[e, 2, 0:8, :] = lax.fori_loop(0, 16, pack, jnp.zeros((8, 128), F32))

    def small_merge(e):
        sf_m[e] = merge(sf_r[e, 2, 8:16, :], sf_r[e, 2, 0:8, :])

    sub16 = lax.broadcasted_iota(jnp.int32, (16, 128), 0)
    lane16 = lax.broadcasted_iota(jnp.int32, (16, 128), 1)

    def small_block(e, x):
        return ext[e, pl.ds(pl.multiple_of(x * 16 + 16, 16), 16), :]

    def small_neighbours(e, x):
        mid = small_block(e, x)
        xp = ext[e, pl.ds(pl.multiple_of(x * 16 + 32, 16), 16), :]
        xm = ext[e, pl.ds(pl.multiple_of(x * 16, 16), 16), :]
        low = jnp.broadcast_to(sf_r[e, 0, pl.ds(x, 1), :], (16, 128))
        high = jnp.broadcast_to(sf_r[e, 1, pl.ds(x, 1), :], (16, 128))
        yp = jnp.where(sub16 == 15, high, pltpu.roll(mid, 15, 0))
        ym = jnp.where(sub16 == 0, low, pltpu.roll(mid, 1, 0))
        sides = jnp.concatenate(
            [pltpu.roll(sf_m[e], 127 - 2 * (2 * x + h), 1) for h in range(2)], axis=0
        )
        zp = jnp.where(lane16 == 127, sides, pltpu.roll(mid, 127, 1))
        zm = jnp.where(lane16 == 0, sides, pltpu.roll(mid, 1, 1))
        return xp, xm, yp, ym, zp, zm

    def small_sum(e, x):
        xp, xm, yp, ym, zp, zm = small_neighbours(e, x)
        return xp + xm + yp + ym + zp + zm

    def mask_block(x):
        bx = x // 8
        both = mrow[pl.ds(2 * bx, 2), :]
        return jnp.where(
            sub16 < 8,
            jnp.broadcast_to(both[0:1, :], (16, 128)),
            jnp.broadcast_to(both[1:2, :], (16, 128)),
        )

    def rows_of(x):
        return pl.ds(pl.multiple_of(x * 16, 16), 16)

    def clear_halos():
        zero_plane = jnp.zeros((16, 8, 128), F32)
        zero_face = jnp.zeros((16, 128), F32)

        def clear(cond, fn):
            pl.when(cond)(fn)

        def span_low():
            for it in range(2):
                field[it, 0, 1:17] = zero_plane
            for e in range(4):
                ext[e, 0:16, :] = zero_face

        def span_high():
            for it in range(2):
                field[it, 17, 1:17] = zero_plane
            for e in range(4):
                ext[e, 272:288, :] = zero_face

        def height_low():
            for it in range(2):
                field[it, 1:17, 0] = zero_plane
            for e in range(4):
                sf_r[e, 0] = zero_face

        def height_high():
            for it in range(2):
                field[it, 1:17, 17] = zero_plane
            for e in range(4):
                sf_r[e, 1] = zero_face

        def depth_low():
            for it in range(2):
                hz_r[it, 0] = jnp.zeros((4, 8, 128), F32)
            for e in range(4):
                sf_r[e, 2, 0:8, :] = jnp.zeros((8, 128), F32)

        def depth_high():
            for it in range(2):
                hz_r[it, 1] = jnp.zeros((4, 8, 128), F32)
            for e in range(4):
                sf_r[e, 2, 8:16, :] = jnp.zeros((8, 128), F32)

        clear(S == 0, span_low)
        clear(S == n_span - 1, span_high)
        clear(H == 0, height_low)
        clear(H == n_height - 1, height_high)
        clear(D == 0, depth_low)
        clear(D == n_depth - 1, depth_high)

    def setup_masked_stiffness():
        phase_in.wait()

        def body(x, _):
            p = small_block(1, x)
            stiff = void_stiffness + (1.0 - void_stiffness) * (p * p * p)
            ext[0, pl.ds(pl.multiple_of(x * 16 + 16, 16), 16), :] = mask_block(x) * stiff
            return 0

        lax.fori_loop(0, 16, body, 0)
        for e in range(2):
            small_faces(e)
            start_all(small_copies(e))

    def setup_coefficients():
        for e in range(2):
            receive_all(small_copies(e))
            small_merge(e)

        def body(x, _):
            p = small_block(1, x)
            stiff = void_stiffness + (1.0 - void_stiffness) * (p * p * p)
            m = mask_block(x)
            half = 0.5 * m
            total = m * spring_rate
            w = []
            for near in small_neighbours(0, x):
                one = half * (jnp.where(near > 0.0, stiff, 0.0) + near)
                total = total + one
                w.append(one)
            at = rows_of(x)
            dco[at, :] = total
            wx[pl.ds(pl.multiple_of(x * 16 + 16, 16), 16), :] = w[0]
            wx[at, :] = w[1]
            wyp[at, :] = w[2]
            wym[at, :] = w[3]
            wzl[at, :] = jnp.where(lane16 == 127, 0.0, w[4])
            wze[at, :] = jnp.where(lane16 == 127, w[4], jnp.where(lane16 == 0, w[5], 0.0))
            b = p / time_step - 0.5 * p * (1.0 - p) * (1.0 - 2.0 * p)
            base[at, :] = b
            ext[2, pl.ds(pl.multiple_of(x * 16 + 16, 16), 16), :] = inverse * (
                b + interface_weight * small_sum(1, x)
            )
            return 0

        lax.fori_loop(0, 16, body, 0)
        small_faces(2)
        start_all(small_copies(2))

    def setup_phase_part():
        receive_all(small_copies(2))
        small_merge(2)

        def body(x, _):
            at = rows_of(x)
            hpart[at, :] = inverse * (base[at, :] + interface_weight * small_sum(2, x))
            return 0

        lax.fori_loop(0, 16, body, 0)

    def load_row(x, y):
        return load_v[pl.ds(x * 16 + y, 8, stride=PITCH), :]

    def side_values(source, x, y):
        n = ((x % 2) * 8 + y % 8) * 4 + (x // 8) * 2 + y // 8
        return pltpu.roll(source, 127 - 2 * n, 1)

    def apply(it, x, y, hz):
        r = pl.ds(x * 16 + y, 1)
        v = field[it, x + 1, y + 1]
        wz = wzl[r, :]
        q = dco[r, :] * v
        q = q - wx[r, :] * field[it, x, y + 1]
        q = q - wx[pl.ds(x * 16 + 16 + y, 1), :] * field[it, x + 2, y + 1]
        q = q - wym[r, :] * field[it, x + 1, y]
        q = q - wyp[r, :] * field[it, x + 1, y + 2]
        q = q - wz * pltpu.roll(v, 127, 1) - pltpu.roll(wz * v, 1, 1)
        q = q - wze[r, :] * side_values(hz, x, y)
        return v, q

    def sums(*accumulated):
        packed = jnp.zeros((8, 128), F32)
        for n, a in enumerate(accumulated):
            packed = jnp.where(lane == n, jnp.sum(a, axis=1, keepdims=True), packed)
        return packed

    def receive_halos(it):
        receive_all(halo_copies(it))
        for g in range(4):
            hz_m[it, g] = merge(hz_r[it, 1, g], hz_r[it, 0, g])

    zero = jnp.zeros((8, 128), F32)
    add = lambda a, b: a + b

    for c in load_in:
        c.wait()
    gather(0, load_row)
    pl.semaphore_wait(barrier, 7 + (n_height - 1) + (n_depth - 1))
    for n in FAR_FIRST:
        a2a_out(0, n).start()
    clear_halos()
    setup_masked_stiffness()
    precondition(0)
    setup_coefficients()
    scatter(0)
    start_all(halo_copies(0))
    setup_phase_part()
    receive_halos(0)

    def first(x, carry):
        rz, zq = carry
        hz = hz_m[0, (x % 8) // 2]
        for y in range(16):
            v, q = apply(0, x, y, hz)
            image[x, y] = q
            rz = rz + load_row(x, y) * v
            zq = zq + v * q
        return rz, zq

    rz, zq = lax.fori_loop(0, 16, first, (zero, zero))
    ar_begin(0, 0, sums(rz, zq))
    gather(1, lambda x, y: image[x, y])
    for n in FAR_FIRST:
        a2a_out(1, n).start()
    ar_begin(0, 1, ar_end(0, 0, add))
    precondition(1)
    ar_begin(0, 2, ar_end(0, 1, add))
    scatter(1)
    start_all(halo_copies(1))
    total = ar_end(0, 2, add)
    rz1 = jnp.broadcast_to(total[:, 0:1], (8, 128))
    zq1 = jnp.broadcast_to(total[:, 1:2], (8, 128))
    alpha1 = rz1 / zq1
    receive_halos(1)

    def second(x, carry):
        rz, zaz, zq = carry
        hz = hz_m[1, (x % 8) // 2]
        for y in range(16):
            w, u = apply(1, x, y, hz)
            q1 = image[x, y]
            z2 = field[0, x + 1, y + 1] - alpha1 * w
            rz = rz + (load_row(x, y) - alpha1 * q1) * z2
            zaz = zaz + z2 * (q1 - alpha1 * u)
            zq = zq + z2 * q1
        return rz, zaz, zq

    ar_begin(1, 0, sums(*lax.fori_loop(0, 16, second, (zero, zero, zero))))
    ar_begin(1, 1, ar_end(1, 0, add))
    ar_begin(1, 2, ar_end(1, 1, add))
    total = ar_end(1, 2, add)
    rz2 = jnp.broadcast_to(total[:, 0:1], (8, 128))
    zaz = jnp.broadcast_to(total[:, 1:2], (8, 128))
    zq2 = jnp.broadcast_to(total[:, 2:3], (8, 128))
    beta = rz2 / rz1
    alpha2 = rz2 / (zaz + beta * (2.0 * zq2 + beta * zq1))
    on_z = alpha1 + alpha2 * (1.0 + beta)
    on_w = -alpha2 * alpha1

    def combine(x, y):
        value = on_z * field[0, x, y] + on_w * field[1, x, y]
        xfield[x, y] = value
        return value

    for x in (0, 17):
        for y in range(1, 17):
            combine(x, y)

    def form(x, _):
        combine(x + 1, 0)
        for y in range(16):
            dx[pl.ds(x * 16 + y, 8, stride=PITCH), :] = combine(x + 1, y + 1)
        combine(x + 1, 17)
        return 0

    lax.fori_loop(0, 16, form, 0)
    for g in range(4):
        hz_m[0, g] = on_z * hz_m[0, g] + on_w * hz_m[1, g]
    disp_out = [
        pltpu.make_async_copy(
            dx.at[pl.ds(l * PITCH, 256)], disp_hbm.at[pl.ds(l * 256, 256)], out_sem.at[l]
        )
        for l in range(8)
    ]
    for c in disp_out:
        c.start()

    def energy(x, peak):
        hz = hz_m[0, (x % 8) // 2]
        for y in range(16):
            r = pl.ds(x * 16 + y, 1)
            v = xfield[x + 1, y + 1]
            e = zero
            for w, near in (
                (wx[r, :], xfield[x, y + 1]),
                (wx[pl.ds(x * 16 + 16 + y, 1), :], xfield[x + 2, y + 1]),
                (wym[r, :], xfield[x + 1, y]),
                (wyp[r, :], xfield[x + 1, y + 2]),
                (wze[r, :], side_values(hz, x, y)),
            ):
                d = v - near
                e = e + jnp.where(w > 0.0, 1.0, 0.0) * (d * d)
            d = v - pltpu.roll(v, 127, 1)
            t = jnp.where(wzl[r, :] > 0.0, 1.0, 0.0) * (d * d)
            e = e + t + pltpu.roll(t, 1, 1)
            erow[r, :] = jnp.sum(e, axis=0, keepdims=True)
        at = rows_of(x)
        p = small_block(1, x)
        s = (-1.5 * (1.0 - void_stiffness)) * (p * p) * mask_block(x) * erow[at, :]
        sens[at, :] = s
        ext[3, pl.ds(pl.multiple_of(x * 16 + 16, 16), 16), :] = inverse * s
        return jnp.maximum(peak, jnp.maximum(-s[0:8, :], -s[8:16, :]))

    peak = lax.fori_loop(0, 16, energy, zero)
    ar_begin(2, 0, peak)
    small_faces(3)
    start_all(small_copies(3))
    sens_out = pltpu.make_async_copy(sens, sens_hbm, out_sem.at[8])
    sens_out.start()
    receive_all(small_copies(3))
    small_merge(3)
    ar_begin(2, 1, ar_end(2, 0, jnp.maximum))

    def slope(x, _):
        at = rows_of(x)
        erow[at, :] = small_block(3, x) + (interface_weight * inverse) * small_sum(3, x)
        return 0

    lax.fori_loop(0, 16, slope, 0)
    ar_begin(2, 2, ar_end(2, 1, jnp.maximum))
    peak = ar_end(2, 2, jnp.maximum)
    peak = jnp.max(jnp.max(peak, axis=1, keepdims=True), axis=0, keepdims=True)
    scale = jnp.broadcast_to(1.0 / (peak + epsilon_peak), (16, 128))

    def finish(x, _):
        at = rows_of(x)
        nxt[at, :] = hpart[at, :] - erow[at, :] * scale
        return 0

    lax.fori_loop(0, 16, finish, 0)
    next_out = pltpu.make_async_copy(nxt, next_hbm, out_sem.at[9])
    next_out.start()

    for it in range(2):
        for n in range(7):
            a2a_out(it, n).wait_send()
            a2a_back(it, n).wait_send()
        sent_all(halo_copies(it))
    for e in range(4):
        sent_all(small_copies(e))
    for k in range(3):
        for stage in range(3):
            for c in ar_copies(k, stage):
                c.wait_send()
    for c in disp_out:
        c.wait()
    sens_out.wait()
    next_out.wait()


def solution(mesh):
    sizes = tuple(mesh.shape[a] for a in AXES)
    dma = pltpu.SemaphoreType.DMA
    vmem = pltpu.VMEM

    def local(load, phase, void, owner, precond):
        any_space = pl.BlockSpec(memory_space=pl.ANY)
        disp, sens, nxt = pl.pallas_call(
            functools.partial(kernel, sizes),
            name="design_step",
            out_shape=(
                jax.ShapeDtypeStruct((2048, 128), F32),
                jax.ShapeDtypeStruct((256, 128), F32),
                jax.ShapeDtypeStruct((256, 128), F32),
            ),
            in_specs=[any_space] * 5,
            out_specs=(any_space,) * 3,
            scratch_shapes=[
                vmem((8 * PITCH, 128), F32),
                vmem((2, 2, 16), jnp.int32),
                vmem((2, 2, 16), jnp.int32),
                vmem((16, 512, 512), BF16),
                vmem((256, 512), BF16),
                vmem((256, 128), BF16),
                vmem((8, 128), F32),
                vmem((512, 512), BF16),
                vmem((512, 128), F32),
                vmem((512, 256), BF16),
                vmem((2, 8, 16, 512), BF16),
                vmem((2, 8, 16, 512), BF16),
                vmem((2, 8, 16, 512), F32),
                vmem((2, 8, 16, 512), F32),
                vmem((2, 18, 18, 8, 128), F32),
                vmem((16, 16, 8, 128), F32),
                vmem((2, 4, 8, 128), F32),
                vmem((2, 2, 4, 8, 128), F32),
                vmem((2, 4, 8, 128), F32),
                vmem((18, 18, 8, 128), F32),
                vmem((8 * PITCH, 128), F32),
                vmem((4, 288, 128), F32),
                vmem((4, 3, 16, 128), F32),
                vmem((4, 3, 16, 128), F32),
                vmem((4, 8, 128), F32),
                vmem((256, 128), F32),
                vmem((272, 128), F32),
                vmem((256, 128), F32),
                vmem((256, 128), F32),
                vmem((256, 128), F32),
                vmem((256, 128), F32),
                vmem((256, 128), F32),
                vmem((256, 128), F32),
                vmem((256, 128), F32),
                vmem((256, 128), F32),
                vmem((256, 128), F32),
                vmem((3, 3, 8, 128), F32),
                vmem((3, 13, 8, 128), F32),
                dma((11,)),
                dma((8,)),
                dma((10,)),
                dma((2, 7)),
                dma((2, 7)),
                dma((2, 7)),
                dma((2, 7)),
                dma((2, 6)),
                dma((2, 6)),
                dma((4, 6)),
                dma((4, 6)),
                dma((3, 13)),
                dma((3, 13)),
            ],
            compiler_params=pltpu.CompilerParams(
                collective_id=0, has_side_effects=True, vmem_limit_bytes=48 * 2**20
            ),
        )(load.reshape(2048, 128), phase.reshape(256, 128), void, owner, precond)
        return (
            disp.reshape(8, 16, 16, 128),
            sens.reshape(16, 16, 128),
            nxt.reshape(16, 16, 128),
        )

    return jax.shard_map(
        local,
        mesh=mesh,
        in_specs=(P(None, *AXES), P(*AXES), P(*AXES), P(*AXES), P(AXES, None, None)),
        out_specs=(P(None, *AXES), P(*AXES), P(*AXES)),
        check_vma=False,
    )
```

profile of v0, /device:TPU:0, one launch (start us, length us, event | category | flops | bytes accessed | tf_op | source)
XLA Modules:
  0.0 77.3 jit_solution(11870238045293984014)
XLA Ops:
  0.6 0.0 copy-start
  0.6 1.2 %copy-done = f32[8,16,16,128]{3,2,1,0:T(8,128)S(1)} copy-done((f32[8,16,16,128]{3,2,1,0:T(8,128)S(1)}, f32[8,16,16,128]{3,2,1,0:T(8,128)}, u32[]{:S(2)}) %copy-start) | copy-done | bytes 1048600
  1.9 0.0 copy-start.1
  1.9 0.9 %copy-done.1 = f32[16,16,128]{2,1,0:T(8,128)S(1)} copy-done((f32[16,16,128]{2,1,0:T(8,128)S(1)}, f32[16,16,128]{2,1,0:T(8,128)}, u32[]{:S(2)}) %copy-start.1) | copy-done | bytes 131096
  2.8 0.0 copy-start.2
  2.8 0.7 copy-done.2
  3.4 0.0 copy-start.3
  3.4 0.7 copy-done.3
  4.1 70.9 %design_step.1 = (f32[2048,128]{1,0:T(8,128)S(1)}, f32[256,128]{1,0:T(8,128)S(1)}, f32[256,128]{1,0:T(8,128)S(1)}) custom-call(f32[2048,128]{1,0:T(8,128)S(1)} %bitcast.5, f32[256,128]{1,0:T(8,128)S(1)} %bitcast.7, s32[2,2,16]{2,1,0:T(2,128)S(1)} %copy-done.2, s32[2,2,16]{2,1,0:T(2,128)S(1)} %copy-done.3, bf16[16,512,512]{2,1,0:T(8,128)(2,1)} %precond_hbm.1), custom_call_target="tpu_custom_call" | custom-call | tf_op jit(solution)/shard_map/design_step/pallas_call | solution.py:716
  75.0 1.0 %copy.11 = f32[8,16,16,128]{3,2,1,0:T(8,128)} copy(f32[8,16,16,128]{3,2,1,0:T(8,128)S(1)} %bitcast.6) | data formatting | bytes 2097152
  76.0 0.7 copy.12
  76.6 0.7 copy.13
Async XLA Ops:
  0.6 1.2 %copy-start = (f32[8,16,16,128]{3,2,1,0:T(8,128)S(1)}, f32[8,16,16,128]{3,2,1,0:T(8,128)}, u32[]{:S(2)}) copy-start(f32[8,16,16,128]{3,2,1,0:T(8,128)} %param.5) | copy-start | bytes 3145732
  1.9 0.9 %copy-start.1 = (f32[16,16,128]{2,1,0:T(8,128)S(1)}, f32[16,16,128]{2,1,0:T(8,128)}, u32[]{:S(2)}) copy-start(f32[16,16,128]{2,1,0:T(8,128)} %param.6) | copy-start | bytes 393220
  2.8 0.7 copy-start.2
  3.4 0.7 copy-start.3
where the time goes:
time: 77.5 us; the launch traced here: 77.3 us
  Pallas kernels  70.9 us (91%)
  local copies, waits for them, and re-layouts  5.77 us (7%)
    pallas_call x1, Pallas kernels, local(): pl.pallas_call(functools.partial(kernel, sizes), name='design_step', out_...  70.9 us
    unnamed x11, local copies, waits for them, and re-layouts  5.77 us

commit v1 on v0

--- a/solution.py
+++ b/solution.py
@@ -41,14 +41,15 @@
 def kernel(
     sizes,
     load_hbm, phase_hbm, void_hbm, owner_hbm, precond_hbm,
-    disp_hbm, sens_hbm, next_hbm,
+    dx, sens, nxt,
     load_v, void_v, owner_v, pre_v, sel, ez, mrow, lb, vs, gbuf,
-    send_a, recv_a, send_r, recv_r, field, image, hz_s, hz_r, hz_m, xfield, dx,
-    ext, sf_s, sf_r, sf_m, dco, wx, wyp, wym, wzl, wze, base, hpart, erow, sens, nxt, ar_s, ar_r,
-    in_sem, pre_sem, out_sem, a2a_ss, a2a_rs, ret_ss, ret_rs, halo_ss, halo_rs,
-    sf_ss, sf_rs, ar_ss, ar_rs,
+    send_a0, send_a1, recv_a0, recv_a1, send_r, recv_r, field, image, quads, hz_s, hz_r, hz_m, wzp,
+    ext, sf_s, sf_r, sf_m, dco, wx, wyp, wym, wzl, wze, base, hpart, slope, rate, ar_s, ar_r,
+    in_sem, pre_sem, a2a_ss, a2a_rs, ret_ss, ret_rs, halo_ss, halo_rs,
+    sf_ss, sf_rs, ar_ss, ar_rs, far_sem,
 ):
     n_span, n_height, n_depth = sizes
+    send_a, recv_a = (send_a0, send_a1), (recv_a0, recv_a1)
     S, H, D = (lax.axis_index(a) for a in AXES)
     yy, core = S // 2, S % 2
     lane = lax.broadcasted_iota(jnp.int32, (8, 128), 1)
@@ -213,7 +214,7 @@
     def a2a_out(it, n):
         to = towards(*PARTNERS[n])
         return span_copy(
-            send_a.at[it, to], recv_a.at[it, S], a2a_ss.at[it, n], a2a_rs.at[it, n], to
+            send_a[it].at[to], recv_a[it].at[S], a2a_ss.at[it, n], a2a_rs.at[it, n], to
         )
 
     def a2a_back(it, n):
@@ -222,38 +223,40 @@
             send_r.at[it, to], recv_r.at[it, S], ret_ss.at[it, n], ret_rs.at[it, n], to
         )
 
+    plane = [(h, d) for h in range(n_height) for d in range(n_depth) if h or d]
+
     def ar_copies(k, stage):
-        if stage == 0:
-            return [
-                span_copy(
-                    ar_s.at[k, 0], ar_r.at[k, n], ar_ss.at[k, n], ar_rs.at[k, n], towards(*p)
+        copies = []
+        for n, p in enumerate(PARTNERS if stage == 0 else plane):
+            at = n + 7 * stage
+            if stage == 0:
+                target = {"span": towards(*p)}
+            else:
+                target = {
+                    "height": lax.rem(H + p[0], n_height),
+                    "depth": lax.rem(D + p[1], n_depth),
+                }
+            copies.append(
+                pltpu.make_async_remote_copy(
+                    src_ref=ar_s.at[k, stage], dst_ref=ar_r.at[k, at],
+                    send_sem=ar_ss.at[k, at], recv_sem=ar_rs.at[k, at],
+                    device_id=target, device_id_type=MESH,
                 )
-                for n, p in enumerate(PARTNERS)
-            ]
-        axis, idx, size = (("height", H, n_height), ("depth", D, n_depth))[stage - 1]
-        first = 7 if stage == 1 else 10
-        return [
-            pltpu.make_async_remote_copy(
-                src_ref=ar_s.at[k, stage], dst_ref=ar_r.at[k, first + d - 1],
-                send_sem=ar_ss.at[k, first + d - 1], recv_sem=ar_rs.at[k, first + d - 1],
-                device_id={axis: lax.rem(idx + d, size)}, device_id_type=MESH,
             )
-            for d in range(1, size)
-        ]
+        return copies
 
     def ar_begin(k, stage, value):
         ar_s[k, stage] = value
-        for c in ar_copies(k, stage):
+        for c in reversed(ar_copies(k, stage)):
             c.start()
 
     def ar_end(k, stage, combine):
         copies = ar_copies(k, stage)
         for c in copies:
             c.wait_recv()
-        first = (0, 7, 10)[stage]
         total = ar_s[k, stage]
         for n in range(len(copies)):
-            total = combine(total, ar_r[k, first + n])
+            total = combine(total, ar_r[k, 7 * stage + n])
         return total
 
     def gather(it, row):
@@ -265,21 +268,34 @@
                         [row(8 * bx + i, 8 * by + j), row(8 * bx + i, 8 * by + j + 1)], axis=0
                     )
                     at = pl.multiple_of(i * 64, 64) + j * 8
-                    lb[pl.ds(at, 16), c * 128 : (c + 1) * 128] = both.astype(BF16)
+                    high = both.astype(BF16)
+                    lb[pl.ds(at, 16), c * 128 : (c + 1) * 128] = high
+                    if it == 1:
+                        low = (both - high.astype(F32)).astype(BF16)
+                        lb[pl.ds(at, 16), 512 + c * 128 : 512 + (c + 1) * 128] = low
             return 0
 
         lax.fori_loop(0, 8, pack, 0)
-        vs[...] = lax.dot_general(
-            lb[...], sel[0:128, :], (((1,), (1,)), ((), ())), preferred_element_type=F32
-        )
+        by_slot = (((1,), (1,)), ((), ()))
+        chosen = lax.dot_general(
+            lb[:, 0:512], sel[0:128, :], by_slot, preferred_element_type=F32
+        )
+        if it == 1:
+            chosen = chosen + lax.dot_general(
+                lb[:, 512:1024], sel[0:128, :], by_slot, preferred_element_type=F32
+            )
+        vs[...] = chosen
 
         def turn(g, _):
             start = pl.multiple_of(g * 128, 128)
             slots = block_transpose([vs[pl.ds(start + 8 * t, 8), :] for t in range(16)])
             for o in range(8):
-                send_a[it, o, :, pl.ds(start, 128)] = jnp.concatenate(
-                    [slots[2 * o], slots[2 * o + 1]], axis=0
-                ).astype(BF16)
+                both = jnp.concatenate([slots[2 * o], slots[2 * o + 1]], axis=0)
+                high = both.astype(BF16)
+                send_a[it][o, 0:16, pl.ds(start, 128)] = high
+                if it == 1:
+                    low = (both - high.astype(F32)).astype(BF16)
+                    send_a[it][o, 16:32, pl.ds(start, 128)] = low
             return 0
 
         lax.fori_loop(0, 4, turn, 0)
@@ -287,18 +303,21 @@
     def own_product(it, src, lhs, out):
         for rank in range(2):
             result = jnp.dot(lhs[...], pre_v[src * 2 + rank], preferred_element_type=F32)
-            out[rank * 8 : rank * 8 + 8, :] = result[rank * 8 : rank * 8 + 8, :]
+            part = result[rank * 8 : rank * 8 + 8, :]
+            if it == 1:
+                part = part + result[16 + rank * 8 : 24 + rank * 8, :]
+            out[rank * 8 : rank * 8 + 8, :] = part
 
     def precondition(it):
         if it == 0:
             pre_in[0].wait()
-        own_product(it, S, send_a.at[it, S], recv_r.at[it, S])
+        own_product(it, S, send_a[it].at[S], recv_r.at[it, S])
         for n in range(7):
             if it == 0:
                 pre_in[n + 1].wait()
             src = sources[n + 1]
             a2a_out(it, n).wait_recv()
-            own_product(it, src, recv_a.at[it, src], send_r.at[it, src])
+            own_product(it, src, recv_a[it].at[src], send_r.at[it, src])
             a2a_back(it, n).start()
 
     def scatter(it):
@@ -343,18 +362,22 @@
     def merge(right, left):
         return jnp.where(lane % 2 == 0, pltpu.roll(right, 127, 1), pltpu.roll(left, 1, 1))
 
+    def unrolled(count, step, body):
+        def several(g, _):
+            for k in range(step):
+                body(g * step + k, 0)
+            return 0
+
+        lax.fori_loop(0, count // step, several, 0)
+
     def small_faces(e):
         for side, y in ((0, 0), (1, 15)):
             sf_s[e, side] = ext[e, pl.ds(16 + y, 16, stride=16), :]
-
-        def pack(x, packed):
-            for h in range(2):
-                n = x * 2 + h
-                rows = ext[e, pl.ds(pl.multiple_of(x * 16 + 16, 8) + 8 * h, 8), :]
-                packed = jnp.where(lane // 2 == n, pltpu.roll(rows, 2 * n + 1, 1), packed)
-            return packed
-
-        sf_s[e, 2, 0:8, :] = lax.fori_loop(0, 16, pack, jnp.zeros((8, 128), F32))
+        parts = [jnp.zeros((8, 128), F32)] * 4
+        for n in range(32):
+            rows = pltpu.roll(ext[e, 16 + 8 * n : 24 + 8 * n, :], 2 * n + 1, 1)
+            parts[n % 4] = jnp.where(lane // 2 == n, rows, parts[n % 4])
+        sf_s[e, 2, 0:8, :] = (parts[0] + parts[1]) + (parts[2] + parts[3])
 
     def small_merge(e):
         sf_m[e] = merge(sf_r[e, 2, 8:16, :], sf_r[e, 2, 0:8, :])
@@ -452,10 +475,11 @@
         def body(x, _):
             p = small_block(1, x)
             stiff = void_stiffness + (1.0 - void_stiffness) * (p * p * p)
-            ext[0, pl.ds(pl.multiple_of(x * 16 + 16, 16), 16), :] = mask_block(x) * stiff
-            return 0
-
-        lax.fori_loop(0, 16, body, 0)
+            m = mask_block(x)
+            ext[0, pl.ds(pl.multiple_of(x * 16 + 16, 16), 16), :] = m * stiff
+            rate[rows_of(x), :] = (-1.5 * (1.0 - void_stiffness)) * (p * p) * m
+
+        unrolled(16, 4, body)
         for e in range(2):
             small_faces(e)
             start_all(small_copies(e))
@@ -489,9 +513,8 @@
             ext[2, pl.ds(pl.multiple_of(x * 16 + 16, 16), 16), :] = inverse * (
                 b + interface_weight * small_sum(1, x)
             )
-            return 0
-
-        lax.fori_loop(0, 16, body, 0)
+
+        unrolled(16, 4, body)
         small_faces(2)
         start_all(small_copies(2))
 
@@ -502,9 +525,8 @@
         def body(x, _):
             at = rows_of(x)
             hpart[at, :] = inverse * (base[at, :] + interface_weight * small_sum(2, x))
-            return 0
-
-        lax.fori_loop(0, 16, body, 0)
+
+        unrolled(16, 4, body)
 
     def load_row(x, y):
         return load_v[pl.ds(x * 16 + y, 8, stride=PITCH), :]
@@ -513,29 +535,79 @@
         n = ((x % 2) * 8 + y % 8) * 4 + (x // 8) * 2 + y // 8
         return pltpu.roll(source, 127 - 2 * n, 1)
 
-    def apply(it, x, y, hz):
+    def local(it, x, y, low, high):
         r = pl.ds(x * 16 + y, 1)
         v = field[it, x + 1, y + 1]
         wz = wzl[r, :]
         q = dco[r, :] * v
-        q = q - wx[r, :] * field[it, x, y + 1]
-        q = q - wx[pl.ds(x * 16 + 16 + y, 1), :] * field[it, x + 2, y + 1]
-        q = q - wym[r, :] * field[it, x + 1, y]
-        q = q - wyp[r, :] * field[it, x + 1, y + 2]
-        q = q - wz * pltpu.roll(v, 127, 1) - pltpu.roll(wz * v, 1, 1)
-        q = q - wze[r, :] * side_values(hz, x, y)
-        return v, q
-
-    def sums(*accumulated):
+        if low:
+            q = q - wx[r, :] * field[it, x, y + 1]
+        if high:
+            q = q - wx[pl.ds(x * 16 + 16 + y, 1), :] * field[it, x + 2, y + 1]
+        if y > 0:
+            q = q - wym[r, :] * field[it, x + 1, y]
+        if y < 15:
+            q = q - wyp[r, :] * field[it, x + 1, y + 2]
+        return v, q - wz * pltpu.roll(v, 127, 1) - pltpu.roll(wz * v, 1, 1)
+
+    def over_planes(body, carry):
+        carry = body(0, carry, False, True)
+        carry = lax.fori_loop(1, 15, lambda x, c: body(x, c, True, True), carry)
+        return body(15, carry, True, False)
+
+    lane_row8 = jnp.broadcast_to(lane_row, (8, 128))
+    sub8 = lax.broadcasted_iota(jnp.int32, (8, 128), 0)
+
+    def as_row(*accumulated):
         packed = jnp.zeros((8, 128), F32)
         for n, a in enumerate(accumulated):
-            packed = jnp.where(lane == n, jnp.sum(a, axis=1, keepdims=True), packed)
-        return packed
+            packed = jnp.where(lane_row8 == 8 * n + sub8, jnp.sum(a, axis=1, keepdims=True), packed)
+        return jnp.sum(packed, axis=0, keepdims=True)
+
+    def from_row(row, n):
+        own = jnp.where(lane_row8 == 8 * n + sub8, jnp.broadcast_to(row, (8, 128)), 0.0)
+        return jnp.broadcast_to(jnp.sum(own, axis=1, keepdims=True), (8, 128))
 
     def receive_halos(it):
         receive_all(halo_copies(it))
         for g in range(4):
             hz_m[it, g] = merge(hz_r[it, 1, g], hz_r[it, 0, g])
+
+    def pack_edge_weights():
+        def body(g, _):
+            packed = [jnp.zeros((8, 128), F32)] * 4
+            for ii in range(2):
+                for c in range(4):
+                    x = 8 * (c // 2) + 2 * g + ii
+                    for j in range(8):
+                        n = (ii * 8 + j) * 4 + c
+                        row = wze[pl.ds(x * 16 + 8 * (c % 2) + j, 1), :]
+                        row = pltpu.roll(jnp.broadcast_to(row, (8, 128)), 2 * n + 1, 1)
+                        packed[c] = jnp.where(lane // 2 == n, row, packed[c])
+            wzp[g] = (packed[0] + packed[1]) + (packed[2] + packed[3])
+            return 0
+
+        lax.fori_loop(0, 4, body, 0)
+
+    def load_sums(rows):
+        first = sub8 < 4
+        out = []
+        for y in range(4):
+            a, b = rows[y], rows[y + 4]
+            out.append(jnp.where(first, a, b) + pltpu.roll(jnp.where(first, b, a), 4, 0))
+        rows = out
+        for half in (2, 1):
+            first = (sub8 % (2 * half)) < half
+            out = []
+            for y in range(half):
+                a, b = rows[y], rows[y + half]
+                other = jnp.where(first, b, a)
+                moved = jnp.where(
+                    first, pltpu.roll(other, 8 - half, 0), pltpu.roll(other, half, 0)
+                )
+                out.append(jnp.where(first, a, b) + moved)
+            rows = out
+        return rows[0]
 
     zero = jnp.zeros((8, 128), F32)
     add = lambda a, b: a + b
@@ -546,46 +618,68 @@
     pl.semaphore_wait(barrier, 7 + (n_height - 1) + (n_depth - 1))
     for n in FAR_FIRST:
         a2a_out(0, n).start()
+    for d in range(1, n_height):
+        pl.semaphore_signal(
+            far_sem, 1, device_id={"height": lax.rem(H + d, n_height)}, device_id_type=MESH
+        )
     clear_halos()
     setup_masked_stiffness()
     precondition(0)
     setup_coefficients()
     scatter(0)
     start_all(halo_copies(0))
-    setup_phase_part()
+
+    def local_first(x, carry, low, high):
+        for y in range(16):
+            image[x, y] = local(0, x, y, low, high)[1]
+        return carry
+
+    over_planes(local_first, 0)
     receive_halos(0)
-
-    def first(x, carry):
-        rz, zq = carry
-        hz = hz_m[0, (x % 8) // 2]
-        for y in range(16):
-            v, q = apply(0, x, y, hz)
-            image[x, y] = q
-            rz = rz + load_row(x, y) * v
-            zq = zq + v * q
-        return rz, zq
-
-    rz, zq = lax.fori_loop(0, 16, first, (zero, zero))
-    ar_begin(0, 0, sums(rz, zq))
-    gather(1, lambda x, y: image[x, y])
+    for y in range(16):
+        image[0, y] = image[0, y] - wx[y : y + 1, :] * field[0, 0, y + 1]
+        image[15, y] = image[15, y] - wx[256 + y : 257 + y, :] * field[0, 17, y + 1]
+
+    def image_row(x, y):
+        r = pl.ds(x * 16 + y, 1)
+        q = image[x, y] - wze[r, :] * side_values(hz_m[0, (x % 8) // 2], x, y)
+        if y == 0:
+            q = q - wym[r, :] * field[0, x + 1, 0]
+        if y == 15:
+            q = q - wyp[r, :] * field[0, x + 1, 17]
+        image[x, y] = q
+        return q
+
+    gather(1, image_row)
     for n in FAR_FIRST:
         a2a_out(1, n).start()
+
+    def first_sums(x, carry):
+        rz, zq = carry
+        for y in range(16):
+            v = field[0, x + 1, y + 1]
+            rz = rz + load_row(x, y) * v
+            zq = zq + image[x, y] * v
+        return rz, zq
+
+    ar_begin(0, 0, as_row(*lax.fori_loop(0, 16, first_sums, (zero, zero))))
+    setup_phase_part()
+    pack_edge_weights()
+    precondition(1)
+    if n_height > 1:
+        pl.semaphore_wait(far_sem, n_height - 1)
     ar_begin(0, 1, ar_end(0, 0, add))
-    precondition(1)
-    ar_begin(0, 2, ar_end(0, 1, add))
     scatter(1)
     start_all(halo_copies(1))
-    total = ar_end(0, 2, add)
-    rz1 = jnp.broadcast_to(total[:, 0:1], (8, 128))
-    zq1 = jnp.broadcast_to(total[:, 1:2], (8, 128))
+    total = ar_end(0, 1, add)
+    rz1 = from_row(total, 0)
+    zq1 = from_row(total, 1)
     alpha1 = rz1 / zq1
-    receive_halos(1)
-
-    def second(x, carry):
+
+    def local_second(x, carry, low, high):
         rz, zaz, zq = carry
-        hz = hz_m[1, (x % 8) // 2]
         for y in range(16):
-            w, u = apply(1, x, y, hz)
+            w, u = local(1, x, y, low, high)
             q1 = image[x, y]
             z2 = field[0, x + 1, y + 1] - alpha1 * w
             rz = rz + (load_row(x, y) - alpha1 * q1) * z2
@@ -593,101 +687,107 @@
             zq = zq + z2 * q1
         return rz, zaz, zq
 
-    ar_begin(1, 0, sums(*lax.fori_loop(0, 16, second, (zero, zero, zero))))
+    rz, zaz, zq = over_planes(local_second, (zero, zero, zero))
+    receive_halos(1)
+
+    def second_direction(x, y):
+        return field[0, x + 1, y + 1] - alpha1 * field[1, x + 1, y + 1]
+
+    outer = zero
+    for y in range(16):
+        outer = outer + second_direction(0, y) * (wx[y : y + 1, :] * field[1, 0, y + 1])
+        outer = outer + second_direction(15, y) * (wx[256 + y : 257 + y, :] * field[1, 17, y + 1])
+        outer = outer + second_direction(y, 0) * (wym[16 * y : 16 * y + 1, :] * field[1, y + 1, 0])
+        outer = outer + second_direction(y, 15) * (
+            wyp[16 * y + 15 : 16 * y + 16, :] * field[1, y + 1, 17]
+        )
+    for g in range(4):
+        outer = outer + (hz_s[0, g] - alpha1 * hz_s[1, g]) * (wzp[g] * hz_m[1, g])
+    ar_begin(1, 0, as_row(rz, zaz + alpha1 * outer, zq))
+
+    def quadratic(x, _):
+        hz0 = hz_m[0, (x % 8) // 2]
+        hz1 = hz_m[1, (x % 8) // 2]
+        for y in range(16):
+            r = pl.ds(x * 16 + y, 1)
+            z, w = field[0, x + 1, y + 1], field[1, x + 1, y + 1]
+            zz = zw = ww = zero
+            for weight, near_z, near_w in (
+                (wx[r, :], field[0, x, y + 1], field[1, x, y + 1]),
+                (wx[pl.ds(x * 16 + 16 + y, 1), :], field[0, x + 2, y + 1], field[1, x + 2, y + 1]),
+                (wym[r, :], field[0, x + 1, y], field[1, x + 1, y]),
+                (wyp[r, :], field[0, x + 1, y + 2], field[1, x + 1, y + 2]),
+                (wze[r, :], side_values(hz0, x, y), side_values(hz1, x, y)),
+            ):
+                solid = weight > 0.0
+                dz = jnp.where(solid, z - near_z, 0.0)
+                dw = jnp.where(solid, w - near_w, 0.0)
+                zz, zw, ww = zz + dz * dz, zw + dz * dw, ww + dw * dw
+            solid = wzl[r, :] > 0.0
+            dz = jnp.where(solid, z - pltpu.roll(z, 127, 1), 0.0)
+            dw = jnp.where(solid, w - pltpu.roll(w, 127, 1), 0.0)
+            uz, uw = pltpu.roll(dz, 1, 1), pltpu.roll(dw, 1, 1)
+            quads[0, x, y] = zz + dz * dz + uz * uz
+            quads[1, x, y] = zw + dz * dw + uz * uw
+            quads[2, x, y] = ww + dw * dw + uw * uw
+        return 0
+
+    lax.fori_loop(0, 8, quadratic, 0)
     ar_begin(1, 1, ar_end(1, 0, add))
-    ar_begin(1, 2, ar_end(1, 1, add))
-    total = ar_end(1, 2, add)
-    rz2 = jnp.broadcast_to(total[:, 0:1], (8, 128))
-    zaz = jnp.broadcast_to(total[:, 1:2], (8, 128))
-    zq2 = jnp.broadcast_to(total[:, 2:3], (8, 128))
+    lax.fori_loop(8, 16, quadratic, 0)
+    total = ar_end(1, 1, add)
+    rz2 = from_row(total, 0)
+    zaz = from_row(total, 1)
+    zq2 = from_row(total, 2)
     beta = rz2 / rz1
     alpha2 = rz2 / (zaz + beta * (2.0 * zq2 + beta * zq1))
     on_z = alpha1 + alpha2 * (1.0 + beta)
     on_w = -alpha2 * alpha1
-
-    def combine(x, y):
-        value = on_z * field[0, x, y] + on_w * field[1, x, y]
-        xfield[x, y] = value
-        return value
-
-    for x in (0, 17):
-        for y in range(1, 17):
-            combine(x, y)
-
-    def form(x, _):
-        combine(x + 1, 0)
-        for y in range(16):
-            dx[pl.ds(x * 16 + y, 8, stride=PITCH), :] = combine(x + 1, y + 1)
-        combine(x + 1, 17)
-        return 0
-
-    lax.fori_loop(0, 16, form, 0)
-    for g in range(4):
-        hz_m[0, g] = on_z * hz_m[0, g] + on_w * hz_m[1, g]
-    disp_out = [
-        pltpu.make_async_copy(
-            dx.at[pl.ds(l * PITCH, 256)], disp_hbm.at[pl.ds(l * 256, 256)], out_sem.at[l]
-        )
-        for l in range(8)
-    ]
-    for c in disp_out:
-        c.start()
-
-    def energy(x, peak):
-        hz = hz_m[0, (x % 8) // 2]
-        for y in range(16):
-            r = pl.ds(x * 16 + y, 1)
-            v = xfield[x + 1, y + 1]
-            e = zero
-            for w, near in (
-                (wx[r, :], xfield[x, y + 1]),
-                (wx[pl.ds(x * 16 + 16 + y, 1), :], xfield[x + 2, y + 1]),
-                (wym[r, :], xfield[x + 1, y]),
-                (wyp[r, :], xfield[x + 1, y + 2]),
-                (wze[r, :], side_values(hz, x, y)),
-            ):
-                d = v - near
-                e = e + jnp.where(w > 0.0, 1.0, 0.0) * (d * d)
-            d = v - pltpu.roll(v, 127, 1)
-            t = jnp.where(wzl[r, :] > 0.0, 1.0, 0.0) * (d * d)
-            e = e + t + pltpu.roll(t, 1, 1)
-            erow[r, :] = jnp.sum(e, axis=0, keepdims=True)
-        at = rows_of(x)
-        p = small_block(1, x)
-        s = (-1.5 * (1.0 - void_stiffness)) * (p * p) * mask_block(x) * erow[at, :]
-        sens[at, :] = s
-        ext[3, pl.ds(pl.multiple_of(x * 16 + 16, 16), 16), :] = inverse * s
-        return jnp.maximum(peak, jnp.maximum(-s[0:8, :], -s[8:16, :]))
-
-    peak = lax.fori_loop(0, 16, energy, zero)
-    ar_begin(2, 0, peak)
+    on_zz, on_zw, on_ww = on_z * on_z, 2.0 * on_z * on_w, on_w * on_w
+
+    def sensitivities(x, peak):
+        for h in range(2):
+            energy = load_sums(
+                [
+                    on_zz * quads[0, x, 8 * h + y]
+                    + on_zw * quads[1, x, 8 * h + y]
+                    + on_ww * quads[2, x, 8 * h + y]
+                    for y in range(8)
+                ]
+            )
+            at = pl.multiple_of(x * 16, 16) + 8 * h
+            s = rate[pl.ds(at, 8), :] * energy
+            sens[pl.ds(at, 8), :] = s
+            ext[3, pl.ds(at + 16, 8), :] = inverse * s
+            peak = jnp.maximum(peak, -s)
+        return peak
+
+    peak = lax.fori_loop(0, 16, sensitivities, zero)
+    ar_begin(2, 0, jnp.max(peak, axis=0, keepdims=True))
     small_faces(3)
     start_all(small_copies(3))
-    sens_out = pltpu.make_async_copy(sens, sens_hbm, out_sem.at[8])
-    sens_out.start()
+
+    def form(x, _):
+        for y in range(16):
+            dx[pl.ds(x * 16 + y, 8, stride=PITCH), :] = (
+                on_z * field[0, x + 1, y + 1] + on_w * field[1, x + 1, y + 1]
+            )
+        return 0
+
+    lax.fori_loop(0, 16, form, 0)
+    ar_begin(2, 1, ar_end(2, 0, jnp.maximum))
     receive_all(small_copies(3))
     small_merge(3)
-    ar_begin(2, 1, ar_end(2, 0, jnp.maximum))
-
-    def slope(x, _):
-        at = rows_of(x)
-        erow[at, :] = small_block(3, x) + (interface_weight * inverse) * small_sum(3, x)
-        return 0
-
-    lax.fori_loop(0, 16, slope, 0)
-    ar_begin(2, 2, ar_end(2, 1, jnp.maximum))
-    peak = ar_end(2, 2, jnp.maximum)
-    peak = jnp.max(jnp.max(peak, axis=1, keepdims=True), axis=0, keepdims=True)
-    scale = jnp.broadcast_to(1.0 / (peak + epsilon_peak), (16, 128))
-
-    def finish(x, _):
-        at = rows_of(x)
-        nxt[at, :] = hpart[at, :] - erow[at, :] * scale
-        return 0
-
-    lax.fori_loop(0, 16, finish, 0)
-    next_out = pltpu.make_async_copy(nxt, next_hbm, out_sem.at[9])
-    next_out.start()
+
+    def slopes(x, _):
+        slope[rows_of(x), :] = small_block(3, x) + (interface_weight * inverse) * small_sum(3, x)
+
+    unrolled(16, 4, slopes)
+    peak = jnp.max(ar_end(2, 1, jnp.maximum), axis=1, keepdims=True)
+    scale = jnp.broadcast_to(1.0 / (peak + epsilon_peak), (8, 128))
+    for n in range(32):
+        at = slice(8 * n, 8 * n + 8)
+        nxt[at, :] = hpart[at, :] - slope[at, :] * scale
 
     for it in range(2):
         for n in range(7):
@@ -697,13 +797,24 @@
     for e in range(4):
         sent_all(small_copies(e))
     for k in range(3):
-        for stage in range(3):
+        for stage in range(2):
             for c in ar_copies(k, stage):
                 c.wait_send()
-    for c in disp_out:
+
+
+def deliver(dx, sens, nxt, disp_hbm, sens_hbm, next_hbm, sem):
+    copies = [
+        pltpu.make_async_copy(
+            dx.at[pl.ds(l * PITCH, 256)], disp_hbm.at[pl.ds(l * 256, 256)], sem.at[l]
+        )
+        for l in range(8)
+    ]
+    copies.append(pltpu.make_async_copy(sens, sens_hbm, sem.at[8]))
+    copies.append(pltpu.make_async_copy(nxt, next_hbm, sem.at[9]))
+    for c in copies:
+        c.start()
+    for c in copies:
         c.wait()
-    sens_out.wait()
-    next_out.wait()
 
 
 def solution(mesh):
@@ -712,17 +823,18 @@
     vmem = pltpu.VMEM
 
     def local(load, phase, void, owner, precond):
-        any_space = pl.BlockSpec(memory_space=pl.ANY)
-        disp, sens, nxt = pl.pallas_call(
+        vmem_space = pl.BlockSpec(memory_space=pltpu.VMEM)
+        hbm_space = pl.BlockSpec(memory_space=pltpu.HBM)
+        results = pl.pallas_call(
             functools.partial(kernel, sizes),
             name="design_step",
             out_shape=(
-                jax.ShapeDtypeStruct((2048, 128), F32),
+                jax.ShapeDtypeStruct((8 * PITCH, 128), F32),
                 jax.ShapeDtypeStruct((256, 128), F32),
                 jax.ShapeDtypeStruct((256, 128), F32),
             ),
-            in_specs=[any_space] * 5,
-            out_specs=(any_space,) * 3,
+            in_specs=[hbm_space] * 5,
+            out_specs=(vmem_space,) * 3,
             scratch_shapes=[
                 vmem((8 * PITCH, 128), F32),
                 vmem((2, 2, 16), jnp.int32),
@@ -731,20 +843,22 @@
                 vmem((256, 512), BF16),
                 vmem((256, 128), BF16),
                 vmem((8, 128), F32),
-                vmem((512, 512), BF16),
+                vmem((512, 1024), BF16),
                 vmem((512, 128), F32),
                 vmem((512, 256), BF16),
-                vmem((2, 8, 16, 512), BF16),
-                vmem((2, 8, 16, 512), BF16),
+                vmem((8, 16, 512), BF16),
+                vmem((8, 32, 512), BF16),
+                vmem((8, 16, 512), BF16),
+                vmem((8, 32, 512), BF16),
                 vmem((2, 8, 16, 512), F32),
                 vmem((2, 8, 16, 512), F32),
                 vmem((2, 18, 18, 8, 128), F32),
                 vmem((16, 16, 8, 128), F32),
+                vmem((3, 16, 16, 8, 128), F32),
                 vmem((2, 4, 8, 128), F32),
                 vmem((2, 2, 4, 8, 128), F32),
                 vmem((2, 4, 8, 128), F32),
-                vmem((18, 18, 8, 128), F32),
-                vmem((8 * PITCH, 128), F32),
+                vmem((4, 8, 128), F32),
                 vmem((4, 288, 128), F32),
                 vmem((4, 3, 16, 128), F32),
                 vmem((4, 3, 16, 128), F32),
@@ -759,12 +873,10 @@
                 vmem((256, 128), F32),
                 vmem((256, 128), F32),
                 vmem((256, 128), F32),
-                vmem((256, 128), F32),
-                vmem((3, 3, 8, 128), F32),
-                vmem((3, 13, 8, 128), F32),
+                vmem((3, 2, 1, 128), F32),
+                vmem((3, 22, 1, 128), F32),
                 dma((11,)),
                 dma((8,)),
-                dma((10,)),
                 dma((2, 7)),
                 dma((2, 7)),
                 dma((2, 7)),
@@ -773,13 +885,30 @@
                 dma((2, 6)),
                 dma((4, 6)),
                 dma((4, 6)),
-                dma((3, 13)),
-                dma((3, 13)),
+                dma((3, 22)),
+                dma((3, 22)),
+                pltpu.SemaphoreType.REGULAR,
             ],
             compiler_params=pltpu.CompilerParams(
                 collective_id=0, has_side_effects=True, vmem_limit_bytes=48 * 2**20
             ),
-        )(load.reshape(2048, 128), phase.reshape(256, 128), void, owner, precond)
+        )(*(
+            pltpu.with_memory_space_constraint(a, pltpu.HBM)
+            for a in (load.reshape(2048, 128), phase.reshape(256, 128), void, owner, precond)
+        ))
+        disp, sens, nxt = pl.pallas_call(
+            deliver,
+            name="deliver",
+            out_shape=(
+                jax.ShapeDtypeStruct((2048, 128), F32),
+                jax.ShapeDtypeStruct((256, 128), F32),
+                jax.ShapeDtypeStruct((256, 128), F32),
+            ),
+            in_specs=[pl.BlockSpec(memory_space=pl.ANY)] * 3,
+            out_specs=(hbm_space,) * 3,
+            scratch_shapes=[dma((10,))],
+            compiler_params=pltpu.CompilerParams(vmem_limit_bytes=2**20),
+        )(*results)
         return (
             disp.reshape(8, 16, 16, 128),
             sens.reshape(16, 16, 128),

time: 77.5 us -> 59.8 us (0.77)
  Pallas kernels: 70.9 us -> 59 us
  local copies, waits for them, and re-layouts: 5.77 us -> 0 us
    pallas_call x1, Pallas kernels: 70.9 us -> 57.9 us  [local(): pl.pallas_call(functools.partial(kernel, sizes), name='design_step', out_...]
    unnamed x11 -> x0, local copies, waits for them, and re-layouts: 5.77 us -> none
    pallas_call x0 -> x1, Pallas kernels: none -> 1.13 us  [local(): pl.pallas_call(deliver, name='deliver', out_shape=(jax.ShapeDtypeStruct((...]
where the time goes in v1:
time: 59.8 us; the launch traced here: 59.7 us
  Pallas kernels  59 us (99%)
  between operations  0.64 us (1%)
    pallas_call x1, Pallas kernels, local(): pl.pallas_call(functools.partial(kernel, sizes), name='design_step', out_...  57.9 us

profile of v1, /device:TPU:0, one launch (start us, length us, event | category | flops | bytes accessed | tf_op | source)
XLA Modules:
  0.0 59.7 jit_solution(11818559050200375942)
XLA Ops:
  0.6 57.9 %design_step.1 = (f32[2112,128]{1,0:T(8,128)S(1)}, f32[256,128]{1,0:T(8,128)S(1)}, f32[256,128]{1,0:T(8,128)S(1)}) custom-call(f32[2048,128]{1,0:T(8,128)} %bitcast.5, f32[256,128]{1,0:T(8,128)} %bitcast.6, s32[2,2,16]{2,1,0:T(2,128)} %void_hbm.1, s32[2,2,16]{2,1,0:T(2,128)} %owner_hbm.1, bf16[16,512,512]{2,1,0:T(8,128)(2,1)} %precond_hbm.1), custom_call_target="tpu_custom_call" | custom-call | tf_op jit(solution)/shard_map/design_step/pallas_call | solution.py:828
  58.5 1.1 %deliver.1 = (f32[2048,128]{1,0:T(8,128)}, f32[256,128]{1,0:T(8,128)}, f32[256,128]{1,0:T(8,128)}) custom-call(f32[2112,128]{1,0:T(8,128)S(1)} %get-tuple-element.9.dx, f32[256,128]{1,0:T(8,128)S(1)} %get-tuple-element.10.sens, f32[256,128]{1,0:T(8,128)S(1)} %get-tuple-element.11.nxt), custom_call_target="tpu_custom_call" | custom-call | tf_op jit(solution)/shard_map/deliver/pallas_call | solution.py:899

commit v2 on v1

--- a/solution.py
+++ b/solution.py
@@ -22,7 +22,6 @@
 PITCH = 264
 
 PARTNERS = ((0, 1), (1, 0), (3, 0), (1, 1), (3, 1), (2, 0), (2, 1))
-FAR_FIRST = (5, 6, 1, 2, 3, 4, 0)
 
 
 def block_transpose(rows):
@@ -42,7 +41,7 @@
     sizes,
     load_hbm, phase_hbm, void_hbm, owner_hbm, precond_hbm,
     dx, sens, nxt,
-    load_v, void_v, owner_v, pre_v, sel, ez, mrow, lb, vs, gbuf,
+    load_v, void_v, owner_v, pre_v, sel, ez, mrow, lb, gbuf,
     send_a0, send_a1, recv_a0, recv_a1, send_r, recv_r, field, image, quads, hz_s, hz_r, hz_m, wzp,
     ext, sf_s, sf_r, sf_m, dco, wx, wyp, wym, wzl, wze, base, hpart, slope, rate, ar_s, ar_r,
     in_sem, pre_sem, a2a_ss, a2a_rs, ret_ss, ret_rs, halo_ss, halo_rs,
@@ -97,49 +96,51 @@
     for c in pre_in:
         c.start()
 
-    void_in.wait()
-    owner_in.wait()
-    o_row = lax.broadcasted_iota(jnp.int32, (8, 16), 0)
-    onehots = []
-    for bx in range(2):
-        own2, solid2 = owner_v[bx], 1 - void_v[bx]
-        for by in range(2):
-            own_row = jnp.broadcast_to(own2[by : by + 1, :], (8, 16))
-            sol_row = jnp.broadcast_to(solid2[by : by + 1, :], (8, 16))
-            onehots.append(jnp.where((own_row == o_row) & (sol_row == 1), 1.0, 0.0))
-    onehot = jnp.concatenate(onehots, axis=0)
-    b_row = lax.broadcasted_iota(jnp.int32, (16, 128), 0)
-    b_lane = lax.broadcasted_iota(jnp.int32, (16, 128), 1) // 8
-    spread = jnp.concatenate(
-        [
-            jnp.where(b_row == b_lane, 1.0, 0.0),
-            jnp.where(b_row < b_lane, 1.0, 0.0),
-            jnp.ones((16, 128), F32),
-        ],
-        axis=1,
-    )
-    counted = jnp.dot(onehot, spread, preferred_element_type=F32)
-    o_col = lax.broadcasted_iota(jnp.int32, (8, 128), 0).astype(F32)
-    row_id = lax.broadcasted_iota(jnp.int32, (128, 128), 0).astype(F32)
     lane_row = lax.broadcasted_iota(jnp.int32, (1, 128), 1)
-    previous = jnp.zeros((8, 128), F32)
-    edge = jnp.full((1, 128), -1.0, F32)
-    for c in range(4):
-        here = counted[c * 8 : c * 8 + 8, 0:128]
-        before = counted[c * 8 : c * 8 + 8, 128:256] + previous
-        previous = previous + counted[c * 8 : c * 8 + 8, 256:384]
-        solid = jnp.sum(here, axis=0, keepdims=True)
-        slot = jnp.sum(here * (2.0 * o_col + before), axis=0, keepdims=True)
-        code = jnp.where(solid > 0.5, slot * 8.0 + (lane_row % 8).astype(F32), -1.0)
-        mrow[c : c + 1, :] = solid
-        picked = jnp.where(row_id == code, 1.0, 0.0).astype(BF16)
-        sel[0:128, c * 128 : (c + 1) * 128] = picked
-        sel[128:256, c * 128 : (c + 1) * 128] = picked
-        edge = jnp.where(lane_row % 8 == 2 * c, jnp.broadcast_to(code[:, 127:128], (1, 128)), edge)
-        edge = jnp.where(lane_row % 8 == 2 * c + 1, jnp.broadcast_to(code[:, 0:1], (1, 128)), edge)
-    picked = jnp.where(row_id == edge, 1.0, 0.0).astype(BF16)
-    ez[0:128, :] = picked
-    ez[128:256, :] = picked
+
+    def plan():
+        void_in.wait()
+        owner_in.wait()
+        o_row = lax.broadcasted_iota(jnp.int32, (8, 16), 0)
+        onehots = []
+        for bx in range(2):
+            own2, solid2 = owner_v[bx], 1 - void_v[bx]
+            for by in range(2):
+                own_row = jnp.broadcast_to(own2[by : by + 1, :], (8, 16))
+                sol_row = jnp.broadcast_to(solid2[by : by + 1, :], (8, 16))
+                onehots.append(jnp.where((own_row == o_row) & (sol_row == 1), 1.0, 0.0))
+        onehot = jnp.concatenate(onehots, axis=0)
+        b_row = lax.broadcasted_iota(jnp.int32, (16, 128), 0)
+        b_lane = lax.broadcasted_iota(jnp.int32, (16, 128), 1) // 8
+        spread = jnp.concatenate(
+            [
+                jnp.where(b_row == b_lane, 1.0, 0.0),
+                jnp.where(b_row < b_lane, 1.0, 0.0),
+                jnp.ones((16, 128), F32),
+            ],
+            axis=1,
+        )
+        counted = jnp.dot(onehot, spread, preferred_element_type=F32)
+        o_col = lax.broadcasted_iota(jnp.int32, (8, 128), 0).astype(F32)
+        row_id = lax.broadcasted_iota(jnp.int32, (128, 128), 0).astype(F32)
+        previous = jnp.zeros((8, 128), F32)
+        edge = jnp.full((1, 128), -1.0, F32)
+        for c in range(4):
+            here = counted[c * 8 : c * 8 + 8, 0:128]
+            before = counted[c * 8 : c * 8 + 8, 128:256] + previous
+            previous = previous + counted[c * 8 : c * 8 + 8, 256:384]
+            solid = jnp.sum(here, axis=0, keepdims=True)
+            slot = jnp.sum(here * (2.0 * o_col + before), axis=0, keepdims=True)
+            code = jnp.where(solid > 0.5, slot * 8.0 + (lane_row % 8).astype(F32), -1.0)
+            mrow[c : c + 1, :] = solid
+            picked = jnp.where(row_id == code, 1.0, 0.0).astype(BF16)
+            sel[0:128, c * 128 : (c + 1) * 128] = picked
+            sel[128:256, c * 128 : (c + 1) * 128] = picked
+            edge = jnp.where(lane_row % 8 == 2 * c, jnp.broadcast_to(code[:, 127:128], (1, 128)), edge)
+            edge = jnp.where(lane_row % 8 == 2 * c + 1, jnp.broadcast_to(code[:, 0:1], (1, 128)), edge)
+        picked = jnp.where(row_id == edge, 1.0, 0.0).astype(BF16)
+        ez[0:128, :] = picked
+        ez[128:256, :] = picked
 
     def halo_copies(it):
         f = field.at[it]
@@ -259,46 +260,36 @@
             total = combine(total, ar_r[k, 7 * stage + n])
         return total
 
-    def gather(it, row):
-        def pack(i, _):
-            for c in range(4):
-                bx, by = c // 2, c % 2
-                for j in range(0, 8, 2):
-                    both = jnp.concatenate(
-                        [row(8 * bx + i, 8 * by + j), row(8 * bx + i, 8 * by + j + 1)], axis=0
-                    )
-                    at = pl.multiple_of(i * 64, 64) + j * 8
-                    high = both.astype(BF16)
-                    lb[pl.ds(at, 16), c * 128 : (c + 1) * 128] = high
-                    if it == 1:
-                        low = (both - high.astype(F32)).astype(BF16)
-                        lb[pl.ds(at, 16), 512 + c * 128 : 512 + (c + 1) * 128] = low
-            return 0
-
-        lax.fori_loop(0, 8, pack, 0)
+    def pack_pair(it, x, y, row):
+        both = jnp.concatenate([row(x, y), row(x, y + 1)], axis=0)
+        high = both.astype(BF16)
+        at, column = (x % 8) * 64 + (y % 8) * 8, ((x // 8) * 2 + y // 8) * 128
+        if not isinstance(x, int):
+            at, column = pl.multiple_of(at, 16), pl.multiple_of(column, 128)
+        lb[pl.ds(at, 16), pl.ds(column, 128)] = high
+        if it == 1:
+            low = (both - high.astype(F32)).astype(BF16)
+            lb[pl.ds(at, 16), pl.ds(column + 512, 128)] = low
+
+    def gather(it):
         by_slot = (((1,), (1,)), ((), ()))
-        chosen = lax.dot_general(
-            lb[:, 0:512], sel[0:128, :], by_slot, preferred_element_type=F32
-        )
-        if it == 1:
-            chosen = chosen + lax.dot_general(
-                lb[:, 512:1024], sel[0:128, :], by_slot, preferred_element_type=F32
+        for g in range(4):
+            rows, lanes = slice(g * 128, g * 128 + 128), slice(g * 128, g * 128 + 128)
+            chosen = lax.dot_general(
+                lb[rows, 0:512], sel[0:128, :], by_slot, preferred_element_type=F32
             )
-        vs[...] = chosen
-
-        def turn(g, _):
-            start = pl.multiple_of(g * 128, 128)
-            slots = block_transpose([vs[pl.ds(start + 8 * t, 8), :] for t in range(16)])
+            if it == 1:
+                chosen = chosen + lax.dot_general(
+                    lb[rows, 512:1024], sel[0:128, :], by_slot, preferred_element_type=F32
+                )
+            slots = block_transpose([chosen[8 * t : 8 * t + 8, :] for t in range(16)])
             for o in range(8):
                 both = jnp.concatenate([slots[2 * o], slots[2 * o + 1]], axis=0)
                 high = both.astype(BF16)
-                send_a[it][o, 0:16, pl.ds(start, 128)] = high
+                send_a[it][o, 0:16, lanes] = high
                 if it == 1:
                     low = (both - high.astype(F32)).astype(BF16)
-                    send_a[it][o, 16:32, pl.ds(start, 128)] = low
-            return 0
-
-        lax.fori_loop(0, 4, turn, 0)
+                    send_a[it][o, 16:32, lanes] = low
 
     def own_product(it, src, lhs, out):
         for rank in range(2):
@@ -324,25 +315,19 @@
         for n in range(7):
             a2a_back(it, n).wait_recv()
 
-        def turn(g, _):
-            start = pl.multiple_of(g * 128, 128)
+        for g in range(4):
             slots = [
-                recv_r[it, s // 2, (s % 2) * 8 : (s % 2) * 8 + 8, pl.ds(start, 128)]
+                recv_r[it, s // 2, (s % 2) * 8 : (s % 2) * 8 + 8, g * 128 : g * 128 + 128]
                 for s in range(16)
             ]
             rows = block_transpose(slots)
             for t in range(0, 16, 2):
                 both = jnp.concatenate([rows[t], rows[t + 1]], axis=0)
                 high = both.astype(BF16)
-                gbuf[pl.ds(start + 8 * t, 16), 0:128] = high
-                gbuf[pl.ds(start + 8 * t, 16), 128:256] = (both - high.astype(F32)).astype(BF16)
-            return 0
-
-        lax.fori_loop(0, 4, turn, 0)
-
-        def place(g, _):
-            start = pl.multiple_of(g * 128, 128)
-            chunk = gbuf[pl.ds(start, 128), :]
+                at = slice(g * 128 + 8 * t, g * 128 + 8 * t + 16)
+                gbuf[at, 0:128] = high
+                gbuf[at, 128:256] = (both - high.astype(F32)).astype(BF16)
+            chunk = gbuf[g * 128 : g * 128 + 128, :]
             cells = jnp.dot(chunk, sel[...], preferred_element_type=F32)
             faces = jnp.dot(chunk, ez[...], preferred_element_type=F32)
             packed = jnp.zeros((8, 128), F32)
@@ -355,9 +340,6 @@
                     ]
                 packed = jnp.where(lane // 8 == t, faces[t * 8 : t * 8 + 8, :], packed)
             hz_s[it, g] = packed
-            return 0
-
-        lax.fori_loop(0, 4, place, 0)
 
     def merge(right, left):
         return jnp.where(lane % 2 == 0, pltpu.roll(right, 127, 1), pltpu.roll(left, 1, 1))
@@ -568,8 +550,8 @@
         own = jnp.where(lane_row8 == 8 * n + sub8, jnp.broadcast_to(row, (8, 128)), 0.0)
         return jnp.broadcast_to(jnp.sum(own, axis=1, keepdims=True), (8, 128))
 
-    def receive_halos(it):
-        receive_all(halo_copies(it))
+    def receive_depth(it):
+        receive_all(halo_copies(it)[4:])
         for g in range(4):
             hz_m[it, g] = merge(hz_r[it, 1, g], hz_r[it, 0, g])
 
@@ -614,9 +596,17 @@
 
     for c in load_in:
         c.wait()
-    gather(0, load_row)
+
+    def pack_load(x, _):
+        for y in range(0, 16, 2):
+            pack_pair(0, x, y, load_row)
+        return 0
+
+    lax.fori_loop(0, 16, pack_load, 0)
+    plan()
+    gather(0)
     pl.semaphore_wait(barrier, 7 + (n_height - 1) + (n_depth - 1))
-    for n in FAR_FIRST:
+    for n in range(7):
         a2a_out(0, n).start()
     for d in range(1, n_height):
         pl.semaphore_signal(
@@ -635,14 +625,15 @@
         return carry
 
     over_planes(local_first, 0)
-    receive_halos(0)
-    for y in range(16):
-        image[0, y] = image[0, y] - wx[y : y + 1, :] * field[0, 0, y + 1]
-        image[15, y] = image[15, y] - wx[256 + y : 257 + y, :] * field[0, 17, y + 1]
+    receive_depth(0)
 
     def image_row(x, y):
         r = pl.ds(x * 16 + y, 1)
         q = image[x, y] - wze[r, :] * side_values(hz_m[0, (x % 8) // 2], x, y)
+        if isinstance(x, int) and x == 0:
+            q = q - wx[r, :] * field[0, 0, y + 1]
+        if isinstance(x, int) and x == 15:
+            q = q - wx[pl.ds(256 + y, 1), :] * field[0, 17, y + 1]
         if y == 0:
             q = q - wym[r, :] * field[0, x + 1, 0]
         if y == 15:
@@ -650,8 +641,24 @@
         image[x, y] = q
         return q
 
-    gather(1, image_row)
-    for n in FAR_FIRST:
+    def pack_inner(x, _):
+        for y in range(2, 14, 2):
+            pack_pair(1, x, y, image_row)
+        return 0
+
+    def pack_rim(x, _):
+        for y in (0, 14):
+            pack_pair(1, x, y, image_row)
+        return 0
+
+    lax.fori_loop(1, 15, pack_inner, 0)
+    receive_all(halo_copies(0)[:4])
+    unrolled(14, 7, lambda x, _: pack_rim(x + 1, 0))
+    for x in (0, 15):
+        for y in range(0, 16, 2):
+            pack_pair(1, x, y, image_row)
+    gather(1)
+    for n in range(7):
         a2a_out(1, n).start()
 
     def first_sums(x, carry):
@@ -688,7 +695,8 @@
         return rz, zaz, zq
 
     rz, zaz, zq = over_planes(local_second, (zero, zero, zero))
-    receive_halos(1)
+    receive_depth(1)
+    receive_all(halo_copies(1)[:4])
 
     def second_direction(x, y):
         return field[0, x + 1, y + 1] - alpha1 * field[1, x + 1, y + 1]
@@ -844,7 +852,6 @@
                 vmem((256, 128), BF16),
                 vmem((8, 128), F32),
                 vmem((512, 1024), BF16),
-                vmem((512, 128), F32),
                 vmem((512, 256), BF16),
                 vmem((8, 16, 512), BF16),
                 vmem((8, 32, 512), BF16),

time: 59.8 us -> 56.2 us (0.940)
  Pallas kernels: 59 us -> 55.4 us
    pallas_call x1, Pallas kernels: 57.9 us -> 54.3 us  [local(): pl.pallas_call(functools.partial(kernel, sizes), name='design_step', out_...]
where the time goes in v2:
time: 56.2 us; the launch traced here: 56.1 us
  Pallas kernels  55.4 us (99%)
  between operations  0.64 us (1%)
    pallas_call x1, Pallas kernels, local(): pl.pallas_call(functools.partial(kernel, sizes), name='design_step', out_...  54.3 us
    pallas_call x1, Pallas kernels, local(): pl.pallas_call(deliver, name='deliver', out_shape=(jax.ShapeDtypeStruct((...  1.13 us

profile of v2, /device:TPU:0, one launch (start us, length us, event | category | flops | bytes accessed | tf_op | source)
XLA Modules:
  0.0 56.1 jit_solution(4077927327738431806)
XLA Ops:
  0.6 54.3 %design_step.1 = (f32[2112,128]{1,0:T(8,128)S(1)}, f32[256,128]{1,0:T(8,128)S(1)}, f32[256,128]{1,0:T(8,128)S(1)}) custom-call(f32[2048,128]{1,0:T(8,128)} %bitcast.5, f32[256,128]{1,0:T(8,128)} %bitcast.6, s32[2,2,16]{2,1,0:T(2,128)} %void_hbm.1, s32[2,2,16]{2,1,0:T(2,128)} %owner_hbm.1, bf16[16,512,512]{2,1,0:T(8,128)(2,1)} %precond_hbm.1), custom_call_target="tpu_custom_call" | custom-call | tf_op jit(solution)/shard_map/design_step/pallas_call | solution.py:836
  54.9 1.1 %deliver.1 = (f32[2048,128]{1,0:T(8,128)}, f32[256,128]{1,0:T(8,128)}, f32[256,128]{1,0:T(8,128)}) custom-call(f32[2112,128]{1,0:T(8,128)S(1)} %get-tuple-element.9.dx, f32[256,128]{1,0:T(8,128)S(1)} %get-tuple-element.10.sens, f32[256,128]{1,0:T(8,128)S(1)} %get-tuple-element.11.nxt), custom_call_target="tpu_custom_call" | custom-call | tf_op jit(solution)/shard_map/deliver/pallas_call | solution.py:906

commit v3 on v2

--- a/solution.py
+++ b/solution.py
@@ -93,9 +93,6 @@
         )
         for n, src in enumerate(sources)
     ]
-    for c in pre_in:
-        c.start()
-
     lane_row = lax.broadcasted_iota(jnp.int32, (1, 128), 1)
 
     def plan():
@@ -260,12 +257,17 @@
             total = combine(total, ar_r[k, 7 * stage + n])
         return total
 
-    def pack_pair(it, x, y, row):
-        both = jnp.concatenate([row(x, y), row(x, y + 1)], axis=0)
+    def pack_pair(it, x, y, upper, lower):
+        both = jnp.concatenate([upper, lower], axis=0)
         high = both.astype(BF16)
-        at, column = (x % 8) * 64 + (y % 8) * 8, ((x // 8) * 2 + y // 8) * 128
-        if not isinstance(x, int):
-            at, column = pl.multiple_of(at, 16), pl.multiple_of(column, 128)
+        if isinstance(x, tuple):
+            bx, pair, side = x
+            at = pl.multiple_of(pair * 128, 128) + side * 64 + (y % 8) * 8
+            column = (bx * 2 + y // 8) * 128
+        else:
+            at, column = (x % 8) * 64 + (y % 8) * 8, ((x // 8) * 2 + y // 8) * 128
+            if not isinstance(x, int):
+                at, column = pl.multiple_of(at, 16), pl.multiple_of(column, 128)
         lb[pl.ds(at, 16), pl.ds(column, 128)] = high
         if it == 1:
             low = (both - high.astype(F32)).astype(BF16)
@@ -284,19 +286,24 @@
                 )
             slots = block_transpose([chosen[8 * t : 8 * t + 8, :] for t in range(16)])
             for o in range(8):
-                both = jnp.concatenate([slots[2 * o], slots[2 * o + 1]], axis=0)
-                high = both.astype(BF16)
-                send_a[it][o, 0:16, lanes] = high
-                if it == 1:
-                    low = (both - high.astype(F32)).astype(BF16)
-                    send_a[it][o, 16:32, lanes] = low
+                pair = slots[2 * o : 2 * o + 2]
+                if it == 0:
+                    send_a[it][o, :, lanes] = jnp.concatenate(pair, axis=0).astype(BF16)
+                    continue
+                for rank in range(2):
+                    high = pair[rank].astype(BF16).astype(F32)
+                    send_a[it][o, rank * 16 : rank * 16 + 16, lanes] = jnp.concatenate(
+                        [high, pair[rank] - high], axis=0
+                    ).astype(BF16)
 
     def own_product(it, src, lhs, out):
         for rank in range(2):
-            result = jnp.dot(lhs[...], pre_v[src * 2 + rank], preferred_element_type=F32)
-            part = result[rank * 8 : rank * 8 + 8, :]
-            if it == 1:
-                part = part + result[16 + rank * 8 : 24 + rank * 8, :]
+            rows = lhs[...] if it == 0 else lhs[rank * 16 : rank * 16 + 16, :]
+            result = jnp.dot(rows, pre_v[src * 2 + rank], preferred_element_type=F32)
+            if it == 0:
+                part = result[rank * 8 : rank * 8 + 8, :]
+            else:
+                part = result[0:8, :] + result[8:16, :]
             out[rank * 8 : rank * 8 + 8, :] = part
 
     def precondition(it):
@@ -596,10 +603,12 @@
 
     for c in load_in:
         c.wait()
+    for c in pre_in:
+        c.start()
 
     def pack_load(x, _):
         for y in range(0, 16, 2):
-            pack_pair(0, x, y, load_row)
+            pack_pair(0, x, y, load_row(x, y), load_row(x, y + 1))
         return 0
 
     lax.fori_loop(0, 16, pack_load, 0)
@@ -627,36 +636,42 @@
     over_planes(local_first, 0)
     receive_depth(0)
 
-    def image_row(x, y):
-        r = pl.ds(x * 16 + y, 1)
-        q = image[x, y] - wze[r, :] * side_values(hz_m[0, (x % 8) // 2], x, y)
-        if isinstance(x, int) and x == 0:
+    def pack_inner(pair, _):
+        sides = hz_m[0, pair]
+        for bx in range(2):
+            for side in range(2):
+                x = 8 * bx + 2 * pair + side
+                for y in range(0, 16, 2):
+                    q = []
+                    for k in range(2):
+                        n = (side * 8 + (y + k) % 8) * 4 + bx * 2 + y // 8
+                        edge = wze[pl.ds(pair * 32 + (8 * bx + side) * 16 + y + k, 1), :]
+                        q.append(image[x, y + k] - edge * pltpu.roll(sides, 127 - 2 * n, 1))
+                        image[x, y + k] = q[k]
+                    pack_pair(1, (bx, pair, side), y, *q)
+        return 0
+
+    lax.fori_loop(0, 4, pack_inner, 0)
+    receive_all(halo_copies(0)[:4])
+
+    def rim_row(x, y):
+        r = slice(16 * x + y, 16 * x + y + 1)
+        q = image[x, y]
+        if x == 0:
             q = q - wx[r, :] * field[0, 0, y + 1]
-        if isinstance(x, int) and x == 15:
-            q = q - wx[pl.ds(256 + y, 1), :] * field[0, 17, y + 1]
+        if x == 15:
+            q = q - wx[256 + y : 257 + y, :] * field[0, 17, y + 1]
         if y == 0:
             q = q - wym[r, :] * field[0, x + 1, 0]
         if y == 15:
             q = q - wyp[r, :] * field[0, x + 1, 17]
-        image[x, y] = q
+        if x in (0, 15) or y in (0, 15):
+            image[x, y] = q
         return q
 
-    def pack_inner(x, _):
-        for y in range(2, 14, 2):
-            pack_pair(1, x, y, image_row)
-        return 0
-
-    def pack_rim(x, _):
-        for y in (0, 14):
-            pack_pair(1, x, y, image_row)
-        return 0
-
-    lax.fori_loop(1, 15, pack_inner, 0)
-    receive_all(halo_copies(0)[:4])
-    unrolled(14, 7, lambda x, _: pack_rim(x + 1, 0))
-    for x in (0, 15):
-        for y in range(0, 16, 2):
-            pack_pair(1, x, y, image_row)
+    for x in range(16):
+        for y in range(0, 16, 2) if x in (0, 15) else (0, 14):
+            pack_pair(1, x, y, rim_row(x, y), rim_row(x, y + 1))
     gather(1)
     for n in range(7):
         a2a_out(1, n).start()
@@ -670,12 +685,12 @@
         return rz, zq
 
     ar_begin(0, 0, as_row(*lax.fori_loop(0, 16, first_sums, (zero, zero))))
-    setup_phase_part()
-    pack_edge_weights()
     precondition(1)
     if n_height > 1:
         pl.semaphore_wait(far_sem, n_height - 1)
     ar_begin(0, 1, ar_end(0, 0, add))
+    setup_phase_part()
+    pack_edge_weights()
     scatter(1)
     start_all(halo_copies(1))
     total = ar_end(0, 1, add)
@@ -743,6 +758,11 @@
     lax.fori_loop(0, 8, quadratic, 0)
     ar_begin(1, 1, ar_end(1, 0, add))
     lax.fori_loop(8, 16, quadratic, 0)
+    for it in range(2):
+        for n in range(7):
+            a2a_out(it, n).wait_send()
+            a2a_back(it, n).wait_send()
+        sent_all(halo_copies(it))
     total = ar_end(1, 1, add)
     rz2 = from_row(total, 0)
     zaz = from_row(total, 1)
@@ -791,23 +811,22 @@
         slope[rows_of(x), :] = small_block(3, x) + (interface_weight * inverse) * small_sum(3, x)
 
     unrolled(16, 4, slopes)
+    for e in range(3):
+        sent_all(small_copies(e))
+    for k in range(2):
+        for stage in range(2):
+            for c in ar_copies(k, stage):
+                c.wait_send()
     peak = jnp.max(ar_end(2, 1, jnp.maximum), axis=1, keepdims=True)
     scale = jnp.broadcast_to(1.0 / (peak + epsilon_peak), (8, 128))
     for n in range(32):
         at = slice(8 * n, 8 * n + 8)
         nxt[at, :] = hpart[at, :] - slope[at, :] * scale
 
-    for it in range(2):
-        for n in range(7):
-            a2a_out(it, n).wait_send()
-            a2a_back(it, n).wait_send()
-        sent_all(halo_copies(it))
-    for e in range(4):
-        sent_all(small_copies(e))
-    for k in range(3):
-        for stage in range(2):
-            for c in ar_copies(k, stage):
-                c.wait_send()
+    sent_all(small_copies(3))
+    for stage in range(2):
+        for c in ar_copies(2, stage):
+            c.wait_send()
 
 
 def deliver(dx, sens, nxt, disp_hbm, sens_hbm, next_hbm, sem):

time: 56.2 us -> 54.8 us (0.975)
  Pallas kernels: 55.4 us -> 54 us
    pallas_call x1, Pallas kernels: 54.3 us -> 52.8 us  [local(): pl.pallas_call(functools.partial(kernel, sizes), name='design_step', out_...]
where the time goes in v3:
time: 54.8 us; the launch traced here: 54.6 us
  Pallas kernels  54 us (99%)
  between operations  0.64 us (1%)
    pallas_call x1, Pallas kernels, local(): pl.pallas_call(functools.partial(kernel, sizes), name='design_step', out_...  52.8 us
    pallas_call x1, Pallas kernels, local(): pl.pallas_call(deliver, name='deliver', out_shape=(jax.ShapeDtypeStruct((...  1.13 us

profile of v3, /device:TPU:0, one launch (start us, length us, event | category | flops | bytes accessed | tf_op | source)
XLA Modules:
  0.0 54.6 jit_solution(12299751218747206701)
XLA Ops:
  0.6 52.8 %design_step.1 = (f32[2112,128]{1,0:T(8,128)S(1)}, f32[256,128]{1,0:T(8,128)S(1)}, f32[256,128]{1,0:T(8,128)S(1)}) custom-call(f32[2048,128]{1,0:T(8,128)} %bitcast.5, f32[256,128]{1,0:T(8,128)} %bitcast.6, s32[2,2,16]{2,1,0:T(2,128)} %void_hbm.1, s32[2,2,16]{2,1,0:T(2,128)} %owner_hbm.1, bf16[16,512,512]{2,1,0:T(8,128)(2,1)} %precond_hbm.1), custom_call_target="tpu_custom_call" | custom-call | tf_op jit(solution)/shard_map/design_step/pallas_call | solution.py:855
  53.5 1.1 %deliver.1 = (f32[2048,128]{1,0:T(8,128)}, f32[256,128]{1,0:T(8,128)}, f32[256,128]{1,0:T(8,128)}) custom-call(f32[2112,128]{1,0:T(8,128)S(1)} %get-tuple-element.9.dx, f32[256,128]{1,0:T(8,128)S(1)} %get-tuple-element.10.sens, f32[256,128]{1,0:T(8,128)S(1)} %get-tuple-element.11.nxt), custom_call_target="tpu_custom_call" | custom-call | tf_op jit(solution)/shard_map/deliver/pallas_call | solution.py:925

commit v4 on v3

--- a/solution.py
+++ b/solution.py
@@ -313,6 +313,10 @@
         for n in range(7):
             if it == 0:
                 pre_in[n + 1].wait()
+            elif n == 6:
+                if n_height > 1:
+                    pl.semaphore_wait(far_sem, n_height - 1)
+                ar_begin(0, 1, ar_end(0, 0, add))
             src = sources[n + 1]
             a2a_out(it, n).wait_recv()
             own_product(it, src, recv_a[it].at[src], send_r.at[it, src])
@@ -601,6 +605,7 @@
     zero = jnp.zeros((8, 128), F32)
     add = lambda a, b: a + b
 
+    plan()
     for c in load_in:
         c.wait()
     for c in pre_in:
@@ -612,7 +617,6 @@
         return 0
 
     lax.fori_loop(0, 16, pack_load, 0)
-    plan()
     gather(0)
     pl.semaphore_wait(barrier, 7 + (n_height - 1) + (n_depth - 1))
     for n in range(7):
@@ -686,9 +690,6 @@
 
     ar_begin(0, 0, as_row(*lax.fori_loop(0, 16, first_sums, (zero, zero))))
     precondition(1)
-    if n_height > 1:
-        pl.semaphore_wait(far_sem, n_height - 1)
-    ar_begin(0, 1, ar_end(0, 0, add))
     setup_phase_part()
     pack_edge_weights()
     scatter(1)

time: 54.8 us -> 54.9 us (level)
  no operation moved by 1% of the time
where the time goes in v4:
time: 54.9 us; the launch traced here: 54.8 us
  Pallas kernels  54.2 us (99%)
  between operations  0.64 us (1%)
    pallas_call x1, Pallas kernels, local(): pl.pallas_call(functools.partial(kernel, sizes), name='design_step', out_...  53 us
    pallas_call x1, Pallas kernels, local(): pl.pallas_call(deliver, name='deliver', out_shape=(jax.ShapeDtypeStruct((...  1.13 us

profile of v4, /device:TPU:0, one launch (start us, length us, event | category | flops | bytes accessed | tf_op | source)
XLA Modules:
  0.0 54.8 jit_solution(8102334443916987578)
XLA Ops:
  0.6 53.0 %design_step.1 = (f32[2112,128]{1,0:T(8,128)S(1)}, f32[256,128]{1,0:T(8,128)S(1)}, f32[256,128]{1,0:T(8,128)S(1)}) custom-call(f32[2048,128]{1,0:T(8,128)} %bitcast.5, f32[256,128]{1,0:T(8,128)} %bitcast.6, s32[2,2,16]{2,1,0:T(2,128)} %void_hbm.1, s32[2,2,16]{2,1,0:T(2,128)} %owner_hbm.1, bf16[16,512,512]{2,1,0:T(8,128)(2,1)} %precond_hbm.1), custom_call_target="tpu_custom_call" | custom-call | tf_op jit(solution)/shard_map/design_step/pallas_call | solution.py:856
  53.7 1.1 %deliver.1 = (f32[2048,128]{1,0:T(8,128)}, f32[256,128]{1,0:T(8,128)}, f32[256,128]{1,0:T(8,128)}) custom-call(f32[2112,128]{1,0:T(8,128)S(1)} %get-tuple-element.9.dx, f32[256,128]{1,0:T(8,128)S(1)} %get-tuple-element.10.sens, f32[256,128]{1,0:T(8,128)S(1)} %get-tuple-element.11.nxt), custom_call_target="tpu_custom_call" | custom-call | tf_op jit(solution)/shard_map/deliver/pallas_call | solution.py:926
